TPU v7x, 512 devices: a 8x2x16 block of a 8x8x16 slice. The times are simulated.
512 devices in a mesh: groups: 2 (over y), seq: 128 (over z, x), tp: 2 (over core).
Axes of the slice: x: 8, y: 2, z: 16, core: 2. Of those that a mesh axis runs over, the one named last changes fastest.
The devices are a block of a 8x8x16 slice.
Arguments:
- stream: bfloat16 [2048, 6144], P(('groups', 'seq'), 'tp'), parts along dimension 0, may hold values from -6 to 6
- queries: bfloat16 [2048, 6144], P(('groups', 'seq'), 'tp'), parts along dimension 0, may hold values from -6 to 6
- key_rows: bfloat16 [2048, 1024], P(('groups', 'seq'), 'tp'), parts along dimension 0, may hold values from -6 to 6
- value_rows: bfloat16 [2048, 1024], P(('groups', 'seq'), 'tp'), parts along dimension 0, may hold values from -6 to 6
- routes: int32 [2048, 2], P(('groups', 'seq')), parts along dimension 0, may hold values from 0 to 3, all different within a row; in each aligned block of 8 rows (0 to 7, 8 to 15, ...) at most 4 rows name the same one
- seq_length: int32 [2], P('groups'), parts along dimension 0, may hold values from 256 to 1024
- norm_gain: float32 [6144], P('tp'), may hold values from 0.25 to 1.75
- router: float32 [6144, 4], P('tp'), may hold values from -0.078125 to 0.078125
- w_up: bfloat16 [6144, 32768], P('tp', 'seq'), may hold values from -0.078125 to 0.078125
- w_down: bfloat16 [32768, 6144], P('seq', 'tp'), may hold values from -0.0625 to 0.0625
- final_gain: float32 [6144], P('tp'), may hold values from 0.25 to 1.75
- value_weight: float32 [6144], P('tp'), may hold values from -0.078125 to 0.078125
- value_bias: float32 [1], replicated, may hold values from -3 to 3
Outputs:
- layer_out: bfloat16 [2048, 6144], P(('groups', 'seq'), 'tp'), parts along dimension 0
- values: float32 [2048], P(('groups', 'seq')), parts along dimension 0
There are 2 independent parts, one for each index of `groups`. A program takes and returns all parts, laid end to end along the dimension named above; an argument that names none is the same for every part. Nothing has to cross between parts.
Inputs may be any that keep to these rules, and one draw needn't show every extreme that they name: `routes`: each row names two different experts; among the rows on one device no expert is named more than 4 times, and some device's rows name some expert exactly 4 times.
All inputs are finite; a program needn't handle non-finite values.
Results may differ from a plain program's by a relative error of at most 0.01.
Values may be sent and summed in bfloat16 or wider, within the bound.
A program may use at most 64 MiB of HBM per device.

v0:
```python
import math

import jax
import jax.numpy as jnp
from jax import lax
from jax.sharding import Mesh
from jax.sharding import PartitionSpec as P

D = 6144
HD = 128
EXPERTS = 4
SEQ = ("seq_0", "seq_1")
GROUPS_SEQ = ("groups", "seq_0", "seq_1")


eps = 1e-05
masked = -1e30


def sent_together(arrays, axis, dim, along):
    both = jnp.concatenate(arrays, axis=along)
    result, at, done = (lax.all_gather(both, axis, axis=dim, tiled=True), 0, [])
    for a in arrays:
        done.append(lax.slice_in_dim(result, at, at + a.shape[along], axis=along))
        at += a.shape[along]
    return tuple(done)


def over_pieces(array, axis):
    pieces = lax.all_gather(array, axis)
    return pieces.sum(axis=0)


def from_everyone(array, axis):
    length = lax.axis_size(axis)
    return lax.all_to_all(
        jnp.broadcast_to(array[None], (length, *array.shape)), axis, 0, 0, tiled=True
    )


def of_everyone(array, axis):
    return from_everyone(array, axis).astype(jnp.float32).sum(axis=0)


def laid_out(pieces, dim):
    lengths = list(pieces.shape[1:])
    lengths[dim] *= pieces.shape[0]
    return jnp.moveaxis(pieces, 0, dim).reshape(lengths)


def stacked_from(array, axes, sequence):
    pieces = array
    for k in sequence:
        pieces = lax.all_gather(pieces, axes[k])
    done = sequence[::-1]
    back = [done.index(k) for k in range(len(axes))]
    pieces = pieces.transpose(*back, *range(len(axes), pieces.ndim))
    return pieces.reshape(-1, *array.shape)


def whole_of(array, axes, sequence, dim):
    return laid_out(stacked_from(array, axes, sequence), dim)


def on_device(
    stream,
    queries,
    key_rows,
    value_rows,
    routes,
    seq_length,
    norm_gain,
    router,
    w_up,
    w_down,
    final_gain,
    value_weight,
    value_bias,
):
    row_count = stream.shape[0]
    half_width = stream.shape[1]
    seq_devices = lax.axis_size(SEQ)
    owners = seq_devices // EXPERTS
    my_index = lax.axis_index(SEQ)
    seq_limit = seq_length[0]
    positions = my_index * row_count + jnp.arange(row_count, dtype=jnp.int32)
    kv_heads = key_rows.shape[1] // HD
    per_group = queries.shape[1] // HD // kv_heads
    grouped = queries.reshape(row_count, kv_heads, per_group, HD)
    inv_root = 1.0 / math.sqrt(HD)
    slot_cap = row_count // 2
    run_max = jnp.full((kv_heads, per_group, row_count), masked, jnp.float32)
    key_block, value_block = sent_together((key_rows, value_rows), SEQ, 0, 1)
    key_count = key_block.shape[0]
    scores = (
        jnp.einsum(
            "qkgd,ckd->kgqc",
            grouped,
            key_block.reshape(key_count, kv_heads, HD),
            preferred_element_type=jnp.float32,
        )
        * inv_root
    )
    key_pos = jnp.arange(key_count, dtype=jnp.int32)
    allowed = (key_pos[None, :] <= positions[:, None]) & (key_pos[None, :] < seq_limit)
    scores = jnp.where(allowed, scores, masked)
    new_max = jnp.maximum(run_max, jnp.max(scores, axis=-1))
    weights = jnp.where(allowed, jnp.exp(scores - new_max[..., None]), 0.0)
    new_sum = jnp.sum(weights, axis=-1)
    update = jnp.einsum(
        "kgqc,ckd->kgqd",
        weights.astype(jnp.bfloat16),
        value_block.reshape(key_count, kv_heads, HD),
        preferred_element_type=jnp.float32,
    )
    attended = (update / new_sum[..., None]).transpose(2, 0, 1, 3).reshape(row_count, half_width)
    hidden = stream.astype(jnp.float32) + attended
    gained = hidden * norm_gain
    squares = jnp.sum(hidden * hidden, axis=1)
    total_sq, raw_logits = (over_pieces(squares, "tp"), over_pieces(jnp.dot(gained, router), "tp"))
    norm_scale = lax.rsqrt(total_sq / D + eps)
    normed = gained * norm_scale[:, None]
    logits = raw_logits * norm_scale[:, None]
    normed_half = normed.astype(jnp.bfloat16)
    expert_ids = jnp.arange(EXPERTS, dtype=jnp.int32)
    chosen = (routes[:, :, None] == expert_ids).astype(jnp.float32)
    picked = jnp.sum(chosen * logits[:, None, :], axis=2)
    gates = jax.nn.sigmoid(picked - picked[:, ::-1])
    flat_hits = chosen.reshape(row_count * 2, EXPERTS)
    earlier = jnp.cumsum(flat_hits, axis=0) - flat_hits
    slot_index = jnp.sum(earlier * flat_hits, axis=1).astype(jnp.int32)
    target = routes.reshape(row_count * 2) * slot_cap + slot_index
    placing = (target[:, None] == jnp.arange(EXPERTS * slot_cap, dtype=jnp.int32)[None, :]).astype(
        jnp.bfloat16
    )
    every_row = lax.all_gather(normed_half, SEQ, axis=0, tiled=True)
    every_route = whole_of(routes, SEQ, (0, 1), 0)
    my_expert = my_index // owners
    row_hits = jnp.sum((every_route == my_expert).astype(jnp.int32), axis=1).reshape(
        seq_devices, row_count
    )
    ranks = jnp.cumsum(row_hits, axis=1) - row_hits
    selector = (
        (ranks[:, :, None] == jnp.arange(slot_cap, dtype=jnp.int32)[None, None, :])
        & (row_hits[:, :, None] > 0)
    ).astype(jnp.bfloat16)
    arrived = jnp.einsum(
        "src,srd->scd",
        selector,
        every_row.reshape(seq_devices, row_count, half_width),
        preferred_element_type=jnp.float32,
    ).astype(jnp.bfloat16)
    lead = arrived.shape[0]
    items = arrived.shape[1]
    flat_rows = arrived.reshape(lead * items, half_width)
    up_part = jnp.dot(flat_rows, w_up, preferred_element_type=jnp.float32)
    up_total = of_everyone(up_part.astype(jnp.bfloat16), "tp").astype(jnp.float32)
    active = jax.nn.silu(up_total).astype(jnp.bfloat16)
    down_part = jnp.dot(active, w_down, preferred_element_type=jnp.float32).astype(jnp.bfloat16)
    partial_out = down_part.reshape(lead, items, half_width)
    returned = lax.all_to_all(partial_out, SEQ, split_axis=0, concat_axis=0, tiled=True)
    summed = jnp.sum(
        returned.reshape(EXPERTS, owners, slot_cap, half_width), axis=1, dtype=jnp.float32
    ).reshape(EXPERTS * slot_cap, half_width)
    fetched = jnp.dot(placing.astype(jnp.float32), summed)
    mixed = jnp.sum(fetched.reshape(row_count, 2, half_width) * gates[:, :, None], axis=1)
    final = hidden + mixed
    sq_part = jnp.sum(final * final, axis=1)
    dot_part = jnp.sum(final * (final_gain * value_weight), axis=1)
    sq_total, dot_total = (over_pieces(sq_part, "tp"), over_pieces(dot_part, "tp"))
    estimate = dot_total * lax.rsqrt(sq_total / D + eps) + value_bias[0]
    estimate = jnp.where(positions < seq_limit, estimate, 0.0)
    return (final.astype(jnp.bfloat16), estimate)


def solution(mesh):
    finer = Mesh(
        mesh.devices.reshape(mesh.shape["groups"], 16, 8, mesh.shape["tp"]),
        ("groups", "seq_0", "seq_1", "tp"),
    )
    placed = (
        P(GROUPS_SEQ, "tp"),
        P(GROUPS_SEQ, "tp"),
        P(GROUPS_SEQ, "tp"),
        P(GROUPS_SEQ, "tp"),
        P(GROUPS_SEQ, None),
        P("groups"),
        P("tp"),
        P("tp", None),
        P("tp", SEQ),
        P(SEQ, "tp"),
        P("tp"),
        P("tp"),
        P(),
    )
    return jax.shard_map(
        on_device,
        mesh=finer,
        in_specs=placed,
        out_specs=(P(GROUPS_SEQ, "tp"), P(GROUPS_SEQ)),
        check_vma=False,
    )
```

profile of v0, /device:TPU:65, one launch (start us, length us, event | category | flops | bytes accessed | tf_op | source)
XLA Modules:
  0.0 552.6 jit_solution(5043075534300548686)
XLA Ops:
  7.3 1.4 pad_maximum_fusion
  9.5 1.3 dynamic-slice
  11.5 169.5 %all-gather.11.cloned.1.call-done = bf16[1024,1024]{1,0:T(8,128)(2,1)} async-done(((bf16[8,1024]{1,0:T(8,128)(2,1)}), bf16[1024,1024]{1,0:T(8,128)(2,1)}) %all-gather.11.cloned.1.call-update) | async-done | bytes 2097168 | tf_op jit(solution)/shard_map/all_gather | solution.py:22
  181.0 2.7 fusion.32
  183.7 2.3 copy.70
  186.0 1.6 fusion.33
  187.6 1.3 copy.71
  189.2 1.7 fusion.8
  191.3 12.9 %all-reduce = f32[16]{0:T(128)S(1)} all-reduce(f32[16]{0:T(128)S(1)} %dynamic-update-slice), channel_id=4, replica_groups=mesh['groups'=2,'seq_0'=16,'seq_1'=8,'tp'=2] {'tp'}, use_global_device_ids=true, to_apply=%add | all-reduce | flops 16 | bytes 128
  205.1 20.9 %all-gather.6 = s32[16,8,2]{1,2,0:T(2,128)S(1)} all-gather(s32[1,8,2]{1,2,0:T(2,128)S(1)} %bitcast.63), channel_id=2, replica_groups=mesh['groups'=2,'seq_0'=16,'seq_1'=8,'tp'=2] {'seq_0'}, dimensions={0}, use_global_device_ids=true | all-gather | bytes 1088 | tf_op jit(solution)/shard_map/all_gather | solution.py:54
  226.0 19.8 %all-gather.1 = s32[128,8,2]{1,2,0:T(2,128)S(1)} all-gather(s32[16,8,2]{1,2,0:T(2,128)S(1)} %all-gather.6), channel_id=3, replica_groups=mesh['groups'=2,'seq_0'=16,'seq_1'=8,'tp'=2] {'seq_1'}, dimensions={0}, use_global_device_ids=true | all-gather | bytes 9216 | tf_op jit(solution)/shard_map/all_gather | solution.py:54
  246.4 96.1 %all-gather.13.cloned.1.call-done = bf16[1024,3072]{1,0:T(8,128)(2,1)} async-done(((bf16[8,3072]{1,0:T(8,128)(2,1)}), bf16[1024,3072]{1,0:T(8,128)(2,1)}) %all-gather.13.cloned.1.call-update) | async-done | bytes 6291472 | tf_op jit(solution)/shard_map/all_gather | solution.py:136
  342.5 6.3 %fusion.2 = bf16[128,4,3072]{2,1,0:T(4,128)(2,1)} fusion(bf16[1024,3072]{1,0:T(8,128)(2,1)} %all-gather.13.cloned.1.call-done, s32[128,8]{1,0:T(8,128)S(1)} %copy.60, pred[128,8]{1,0:T(8,128)(4,1)S(1)} %copy.61), kind=kOutput, calls=%fused_computation.3 | convolution fusion | flops 26746880 | bytes 9442304 | tf_op jit(solution)/shard_map/src,srd->scd/dot_general | solution.py:147
  348.8 5.9 %reshape.135 = bf16[512,3072]{1,0:T(8,128)(2,1)} reshape(bf16[128,4,3072]{2,1,0:T(4,128)(2,1)} %fusion.2) | data formatting | bytes 6291456 | tf_op jit(solution)/shard_map/reshape | solution.py:155
  354.7 3.3 convolution_convert_fusion.1
  358.1 11.9 %all_to_all.10 = bf16[2,512,256]{2,1,0:T(8,128)(2,1)S(1)} all-to-all(bf16[2,512,256]{2,1,0:T(8,128)(2,1)S(1)} %broadcast_in_dim.23), channel_id=1, replica_groups=mesh['groups'=2,'seq_0'=16,'seq_1'=8,'tp'=2] {'tp'}, dimensions={0} | all-to-all | bytes 1048576 | tf_op jit(solution)/shard_map/all_to_all | solution.py:36
  370.1 2.7 convolution_convert_fusion
  372.8 6.1 %reshape.136 = bf16[128,4,3072]{2,1,0:T(4,128)(2,1)} reshape(bf16[512,3072]{1,0:T(8,128)(2,1)} %convolution_convert_fusion) | data formatting | bytes 6291456 | tf_op jit(solution)/shard_map/reshape | solution.py:160
  378.9 17.0 %all-to-all-start.1 = ((bf16[128,4,3072]{2,1,0:T(4,128)(2,1)}), bf16[128,4,3072]{2,1,0:T(4,128)(2,1)}, u32[]{:S(2)}, u32[]{:S(2)}) async-start(bf16[128,4,3072]{2,1,0:T(4,128)(2,1)} %reshape.136), calls=%async_computation.1 | async-start | bytes 6291456 | tf_op jit(solution)/shard_map/all_to_all | solution.py:161
  397.4 2.2 all-gather.7
  399.6 132.8 %all-to-all-done.1 = bf16[128,4,3072]{2,1,0:T(4,128)(2,1)} async-done(((bf16[128,4,3072]{2,1,0:T(4,128)(2,1)}), bf16[128,4,3072]{2,1,0:T(4,128)(2,1)}, u32[]{:S(2)}, u32[]{:S(2)}) %all-to-all-start.1) | async-done | bytes 3145760 | tf_op jit(solution)/shard_map/all_to_all | solution.py:161
  532.5 3.2 convert_reduce_fusion
  535.9 0.8 multiply_reduce_fusion
  537.1 7.9 %all-reduce.3 = (f32[16]{0:T(128)S(1)}, f32[16]{0:T(128)S(1)}) all-reduce(f32[16]{0:T(128)S(1)} %dynamic-update-slice.1, f32[16]{0:T(128)S(1)} %dynamic-update-slice.2), channel_id=6, replica_groups=mesh['groups'=2,'seq_0'=16,'seq_1'=8,'tp'=2] {'tp'}, use_global_device_ids=true, to_apply=%add.1 | all-reduce | flops 32 | bytes 256
  (69 shorter events, 4.9 us)
Async XLA Ops:
  7.2 362.9 %copy-start = (bf16[256,3072]{1,0:T(8,128)(2,1)S(1)}, bf16[256,3072]{1,0:T(8,128)(2,1)}, u32[]{:S(2)}) copy-start(bf16[256,3072]{1,0:T(8,128)(2,1)} %param.22) | copy-start | bytes 4718596
  7.2 173.8 %all-gather.11.cloned.1.call-start = ((), (), s32[]{:S(2)}) async-start(), calls=%async_computation.2 | async-start | bytes 2113536 | tf_op jit(solution)/shard_map/all_gather | solution.py:22
  8.7 333.8 %all-gather.13.cloned.1.call-start = ((), (), s32[]{:S(2)}) async-start(), calls=%async_computation.3 | async-start | bytes 6340608 | tf_op jit(solution)/shard_map/all_gather | solution.py:136
  11.5 174.5 %copy-start.7 = (bf16[8,3072]{1,0:T(8,128)(2,1)S(1)}, bf16[8,3072]{1,0:T(8,128)(2,1)}, u32[]{:S(2)}) copy-start(bf16[8,3072]{1,0:T(8,128)(2,1)} %param.14) | copy-start | bytes 147460
  187.5 3.4 copy-start.1
  187.6 16.7 %copy-start.2 = (f32[3072]{0:T(1024)S(1)}, f32[3072]{0:T(1024)}, u32[]{:S(2)}) copy-start(f32[3072]{0:T(1024)} %param.19) | copy-start | bytes 36868
  187.6 17.5 %copy-start.6 = (s32[8,2]{0,1:T(2,128)S(1)}, s32[8,2]{0,1:T(2,128)}, u32[]{:S(2)}) copy-start(s32[8,2]{0,1:T(2,128)} %param.17) | copy-start | bytes 196
  378.9 18.3 %copy-start.4 = (f32[3072]{0:T(1024)S(1)}, f32[3072]{0:T(1024)}, u32[]{:S(2)}) copy-start(f32[3072]{0:T(1024)} %param.23) | copy-start | bytes 36868
  378.9 18.3 %copy-start.5 = (f32[3072]{0:T(1024)S(1)}, f32[3072]{0:T(1024)}, u32[]{:S(2)}) copy-start(f32[3072]{0:T(1024)} %param.24) | copy-start | bytes 36868
  378.9 18.3 %copy-start.3 = (f32[3072,4]{0,1:T(4,128)S(1)}, f32[3072,4]{0,1:T(4,128)}, u32[]{:S(2)}) copy-start(f32[3072,4]{0,1:T(4,128)} %param.20) | copy-start | bytes 147460
  378.9 153.6 %all-to-all-start.1 = ((bf16[128,4,3072]{2,1,0:T(4,128)(2,1)}), bf16[128,4,3072]{2,1,0:T(4,128)(2,1)}, u32[]{:S(2)}, u32[]{:S(2)}) async-start(bf16[128,4,3072]{2,1,0:T(4,128)(2,1)} %reshape.136), calls=%async_computation.1 | async-start | bytes 6291456 | tf_op jit(solution)/shard_map/all_to_all | solution.py:161
Sparse Core Ops, SparseCore 0:
  11.6 169.3 all-gather.10
  205.2 137.3 all-gather.12
where the time goes:
time: 553 us
  waiting for transfers between devices  399 us (72%)
  blocking collectives  75.5 us (14%)
  local copies, waits for them, and re-layouts  21.4 us (4%)
  starting transfers between devices  17.1 us (3%)
  between operations  16.3 us (3%)
  matrix products  15.9 us (3%)
  other arithmetic  7.87 us (1%)
    all_gather x1, waiting for transfers between devices, sent_together(): result, at, done = (lax.all_gather(both, axis, axis=dim, tiled=True), 0, [])  170 us
    all_to_all x1, waiting for transfers between devices, on_device(): lax.all_to_all(partial_out, SEQ, split_axis=0, concat_axis=0, tiled=True)  133 us
    all_gather x1, waiting for transfers between devices, on_device(): every_row = lax.all_gather(normed_half, SEQ, axis=0, tiled=True)  96.1 us
    all_gather x2, blocking collectives, stacked_from(): pieces = lax.all_gather(pieces, axes[k])  40.7 us
    unnamed x2, blocking collectives  20.7 us
    all_to_all x1, starting transfers between devices, on_device(): lax.all_to_all(partial_out, SEQ, split_axis=0, concat_axis=0, tiled=True)  17 us
    all_to_all x1, blocking collectives, from_everyone(): lax.all_to_all(jnp.broadcast_to(array[None], (length, *array.shape)), axi...  11.9 us
  transfers between devices with their start and end apart: 3, of which 3 were waited for; matrix products, arithmetic and copies ran while one was open for 1% of the time, Pallas kernels for 0%

commit v1 on v0

v1 whole, which is shorter than its diff:
```python
import functools
import math

import jax
import jax.numpy as jnp
from jax import lax
from jax.experimental import pallas as pl
from jax.experimental.pallas import tpu as pltpu
from jax.sharding import Mesh
from jax.sharding import PartitionSpec as P

HD = 128
EXPERTS = 4
META = 128
SEQ = ("z", "x")
GROUPS_SEQ = ("groups", "z", "x")
eps = 1e-05
masked = -1e30
f32 = jnp.float32
bf16 = jnp.bfloat16


def lane_sum(a):
    return jnp.sum(a, axis=1, keepdims=True)


def kernel(
    dims,
    queries,
    key_rows,
    value_rows,
    stream,
    routes,
    seq_length,
    norm_gain,
    router,
    w_up_hbm,
    w_down_hbm,
    value_gain,
    value_bias,
    layer_out,
    values,
    kv,
    rows_z,
    rows_x,
    hidden,
    w_up,
    w_down,
    stats,
    stats_in,
    ups,
    ups_in,
    acts,
    parts,
    sums_r,
    sums_l,
    recv_r,
    recv_l,
    sums_z,
    recv_z,
    local_sem,
    zsend,
    xsend,
    zrecv,
    xrecv,
    tsend,
    trecv,
    usend,
    urecv,
):
    nz, nx, full_width = dims
    units, hops = nz // 2, nx // 2
    z, x, t = lax.axis_index("z"), lax.axis_index("x"), lax.axis_index("tp")
    up, down = {"z": lax.rem(z + 1, nz)}, {"z": lax.rem(z + nz - 1, nz)}
    right, left = {"x": lax.rem(x + 1, nx)}, {"x": lax.rem(x + nx - 1, nx)}
    twin = {"tp": 1 - t}
    count, width = stream.shape
    kv_width = key_rows.shape[1]

    def remote(src, dst, send, recv, to):
        return pltpu.make_async_remote_copy(
            src_ref=src, dst_ref=dst, send_sem=send, recv_sem=recv, device_id=to,
            device_id_type=pl.DeviceIdType.MESH,
        )

    key_copy = pltpu.make_async_copy(key_rows, kv.at[0, x, 0, :, pl.ds(0, kv_width)], local_sem.at[0])
    value_copy = pltpu.make_async_copy(
        value_rows, kv.at[0, x, 0, :, pl.ds(kv_width, kv_width)], local_sem.at[1]
    )
    up_copy = pltpu.make_async_copy(w_up_hbm, w_up, local_sem.at[2])
    down_copy = pltpu.make_async_copy(w_down_hbm, w_down, local_sem.at[3])
    key_copy.start()
    value_copy.start()
    up_copy.start()
    down_copy.start()
    barrier = pltpu.get_barrier_semaphore()
    for peer in (up, down, right, left, twin):
        pl.semaphore_signal(barrier, inc=1, device_id=peer, device_id_type=pl.DeviceIdType.MESH)
    key_copy.wait()
    value_copy.wait()
    pl.semaphore_wait(barrier, 5)

    def gather(phase, z_at, x_at, chosen, finish):
        def z_copy(way, u):
            if way == 0:
                return remote(z_at(u - 1, 0), z_at(u, 0), zsend.at[0, u], zrecv.at[phase, 0, u], down)
            return remote(z_at(u - 1, 1), z_at(u, 1), zsend.at[1, u], zrecv.at[phase, 1, u], up)

        def z_first():
            return remote(z_at(0, 0), z_at(0, 1), zsend.at[1, 0], zrecv.at[phase, 1, 0], up)

        def x_copy(way, u, h):
            back = nx - (h - 1) if way == 0 else h - 1
            at = x_at(u, lax.rem(x + back, nx))
            return remote(
                at, at, xsend.at[way, u, h - 1], xrecv.at[phase, way, u, h - 1], right if way == 0 else left
            )

        def x_arrival(way, u, h):
            back = nx - h if way == 0 else h
            at = x_at(u, lax.rem(x + back, nx))
            return remote(
                at, at, xsend.at[way, u, h - 1], xrecv.at[phase, way, u, h - 1], right if way == 0 else left
            )

        z_first().start()
        z_copy(0, 1).start()

        def slot(step, carry):
            @pl.when(step < units)
            def _():
                u = step

                @pl.when(u > 0)
                def _():
                    z_copy(0, u).wait_recv()
                    z_copy(1, u).wait_recv()

                @pl.when(u == 0)
                def _():
                    z_first().wait_recv()

                @pl.when(u < units - 1)
                def _():
                    z_copy(1, u + 1).start()

                @pl.when((u > 0) & (u < units - 1))
                def _():
                    z_copy(0, u + 1).start()

                chosen(u)
                x_copy(0, u, 1).start()
                x_copy(1, u, 1).start()

            for h in range(1, hops):
                u = step - h

                @pl.when((u >= 0) & (u < units))
                def _():
                    for way in (0, 1):
                        x_arrival(way, u, h).wait_recv()
                        if h < hops - 1:
                            x_copy(way, u, h + 1).start()
                        else:

                            @pl.when(lax.rem(u, 2) == way)
                            def _():
                                x_copy(way, u, h + 1).start()

            u = step - hops

            @pl.when(u >= 0)
            def _():
                for way in (0, 1):

                    @pl.when(lax.rem(u, 2) == way)
                    def _():
                        x_arrival(way, u, hops).wait_recv()

                finish(u)

            return carry

        lax.fori_loop(0, units + hops, slot, 0)

        def drain(u, carry):
            @pl.when(u > 0)
            def _():
                z_copy(0, u).wait_send()
                z_copy(1, u).wait_send()

            @pl.when(u == 0)
            def _():
                z_first().wait_send()

            for way in (0, 1):
                for h in range(1, hops):
                    x_copy(way, u, h).wait_send()

                @pl.when(lax.rem(u, 2) == way)
                def _():
                    x_copy(way, u, hops).wait_send()

            return carry

        lax.fori_loop(0, units, drain, 0)

    gather(
        0,
        lambda u, half: kv.at[u, x, half],
        lambda u, source: kv.at[u, source],
        lambda u: None,
        lambda u: None,
    )

    heads = kv_width // HD
    per_group = width // kv_width
    keys = nz * nx * count
    limit = seq_length[0]
    n = lax.broadcasted_iota(jnp.int32, (1, keys), 1)
    per_unit = nx * 2 * count
    key_u, rest = n // per_unit, lax.rem(n, per_unit)
    key_x, rest = rest // (2 * count), lax.rem(rest, 2 * count)
    key_half, key_r = rest // count, lax.rem(rest, count)
    key_z = lax.rem(jnp.where(key_half == 0, z + key_u, z - key_u - 1 + nz), nz)
    key_pos = (key_z * nx + key_x) * count + key_r
    token = lax.broadcasted_iota(jnp.int32, (count, 1), 0)
    my_pos = (z * nx + x) * count + token
    ok = (key_pos <= my_pos) & (key_pos < limit)
    allowed = jnp.concatenate([ok.astype(f32)] * per_group, axis=0) > 0.5
    for head in range(heads):
        q = jnp.concatenate(
            [
                queries[:, (head * per_group + j) * HD : (head * per_group + j + 1) * HD].astype(f32)
                for j in range(per_group)
            ],
            axis=0,
        ).astype(bf16)
        k = kv[:, :, :, :, head * HD : (head + 1) * HD].reshape(keys, HD)
        v = kv[:, :, :, :, kv_width + head * HD : kv_width + (head + 1) * HD].reshape(keys, HD)
        s = lax.dot_general(q, k, (((1,), (1,)), ((), ())), preferred_element_type=f32) * (1.0 / math.sqrt(HD))
        s = jnp.where(allowed, s, masked)
        p = jnp.where(allowed, jnp.exp(s - jnp.max(s, axis=1, keepdims=True)), 0.0)
        o = jnp.dot(p.astype(bf16), v, preferred_element_type=f32) / lane_sum(p)
        for j in range(per_group):
            at = slice((head * per_group + j) * HD, (head * per_group + j + 1) * HD)
            hidden[:, at] = stream[:, at].astype(f32) + o[j * count : (j + 1) * count]

    def both(index, message):
        stats[index] = message
        copy = remote(stats.at[index], stats_in.at[index], tsend.at[index], trecv.at[index], twin)
        copy.start()
        copy.wait()
        return message + stats_in[index]

    lane = lax.broadcasted_iota(jnp.int32, (count, META), 1)
    row = lax.broadcasted_iota(jnp.int32, (count, META), 0)
    h_all = hidden[...]
    gained = h_all * norm_gain[...]
    raw = jnp.dot(gained, router[...], preferred_element_type=f32, precision=lax.Precision.HIGHEST)
    message = jnp.where(lane == EXPERTS, lane_sum(h_all * h_all), 0.0)
    for e in range(EXPERTS):
        message = jnp.where(lane == e, raw[:, e : e + 1], message)
    total = both(0, message)
    sq = lane_sum(jnp.where(lane == EXPERTS, total, 0.0))
    scale = lax.rsqrt(sq / full_width + eps)
    logits = total * scale
    first, second = routes[:, 0:1], routes[:, 1:2]
    hit_a, hit_b = lane == first, lane == second
    gap = lane_sum(jnp.where(hit_a, logits, 0.0)) - lane_sum(jnp.where(hit_b, logits, 0.0))
    gate_a, gate_b = 1.0 / (1.0 + jnp.exp(-gap)), 1.0 / (1.0 + jnp.exp(gap))
    hits = jnp.where(hit_a | hit_b, 1.0, 0.0)
    rank = jnp.zeros((count, META), f32)
    for i in range(count - 1):
        rank = rank + jnp.where(row > i, jnp.broadcast_to(hits[i : i + 1], (count, META)), 0.0)
    place = jnp.where(hits > 0.5, rank + 1.0, 0.0)
    meta = place
    for base, hit, gate in ((0, first, gate_a), (0, second, gate_b)):
        high = gate.astype(bf16).astype(f32)
        meta = jnp.where(lane == hit + EXPERTS, high, meta)
        meta = jnp.where(lane == hit + 2 * EXPERTS, gate - high, meta)
    rows_z[0, 0, :, :width] = (gained * scale).astype(bf16)
    rows_z[0, 0, :, width:] = meta.astype(bf16)

    my_expert = z // (nz // EXPERTS)

    def column(info, which):
        return lane_sum(jnp.where(lane == which * EXPERTS + my_expert, info, 0.0))

    slots = count // 2

    def choose(u):
        out = jnp.zeros((count, width), f32)
        for half in (0, 1):
            block = rows_z[u, half].astype(f32)
            places = jnp.broadcast_to(column(block[:, width:], 0), (count, META))
            for i in range(count):
                want = jnp.broadcast_to(places[i : i + 1], (count, META)) + (slots * half)
                mine = (row + 1).astype(f32) == want
                mine = jnp.where(mine & (want > slots * half + 0.5), 1.0, 0.0)
                out = out + mine[:, 0:1] * block[i : i + 1, :width]
        rows_x[u, x] = out.astype(bf16)

    def ups_copy(u):
        return remote(ups.at[u], ups_in.at[u], usend.at[u], urecv.at[u], twin)

    def activate(u):
        ups_copy(u).wait_recv()
        v = ups[u] + ups_in[u]
        acts[u] = (v / (1.0 + jnp.exp(-v))).astype(bf16)

    def project(u):
        @pl.when(u == 0)
        def _():
            up_copy.wait()

        got = rows_x[u].reshape(nx * count, width)
        ups[u] = jnp.dot(got, w_up[...], preferred_element_type=f32)
        ups_copy(u).start()

    gather(1, lambda u, half: rows_z.at[u, half], lambda u, source: rows_x.at[u, source], choose, project)
    down_copy.wait()

    def act_all(u, carry):
        activate(u)
        ups_copy(u).wait_send()
        return carry

    lax.fori_loop(0, units, act_all, 0)

    def r_copy(way, u, k, src):
        return remote(
            src,
            (recv_r if way == 0 else recv_l).at[u, k],
            xsend.at[way, u, k],
            xrecv.at[2, way, u, k],
            right if way == 0 else left,
        )

    def own(way, u, k):
        ahead = hops - k
        return parts.at[u, lax.rem(x + (ahead if way == 0 else nx - ahead), nx)]

    def zr_copy(way, u):
        return remote(
            sums_z.at[way, u], recv_z.at[way, u], zsend.at[way, u], zrecv.at[2, way, u], up if way == 0 else down
        )

    def home(u):
        both_ways = recv_r[u, hops - 1].astype(f32) + recv_l[u, hops - 1].astype(f32)
        done = parts[u, x].astype(f32) + both_ways
        for half in (0, 1):
            info = rows_z[u, half, :, width:].astype(f32)
            places = column(info, 0)
            gate = column(info, 1) + column(info, 2)
            mix = jnp.zeros((count, width), f32)
            for i in range(slots):
                weight = jnp.where(places == float(i + 1), gate, 0.0)
                mix = mix + weight * done[half * slots + i : half * slots + i + 1]
            sums_z[half, u] = mix.astype(bf16)

            @pl.when(u < units - 1)
            def _():
                zr_copy(half, u + 1).wait_recv()
                total = mix + recv_z[half, u + 1].astype(f32)
                sums_z[half, u] = total.astype(bf16)

                if half == 0:

                    @pl.when(u == 0)
                    def _():
                        hidden[...] = hidden[...] + total

            if half == 0:

                @pl.when(u > 0)
                def _():
                    zr_copy(0, u).start()

            else:
                zr_copy(1, u).start()

    def scatter(step, carry):
        @pl.when(step < units)
        def _():
            u = units - 1 - step
            made = jnp.dot(acts[u], w_down[...], preferred_element_type=f32)
            for d in range(nx):
                parts[u, d] = made[d * count : (d + 1) * count].astype(bf16)
            for way in (0, 1):

                @pl.when(lax.rem(u, 2) == way)
                def _():
                    r_copy(way, u, 0, own(way, u, 0)).start()

        for k in range(1, hops):
            u = units - 1 - (step - k)

            @pl.when((u >= 0) & (u < units))
            def _():
                for way, recv, sums in ((0, recv_r, sums_r), (1, recv_l, sums_l)):

                    def add():
                        r_copy(way, u, k - 1, own(way, u, k - 1)).wait_recv()
                        total = recv[u, k - 1].astype(f32) + own(way, u, k)[...].astype(f32)
                        sums[u, k] = total.astype(bf16)
                        r_copy(way, u, k, sums.at[u, k]).start()

                    if k > 1:
                        add()
                    else:
                        pl.when(lax.rem(u, 2) == way)(add)

                        @pl.when(lax.rem(u, 2) != way)
                        def _():
                            r_copy(way, u, k, own(way, u, k)).start()

        u = units - 1 - (step - hops)

        @pl.when(u < units)
        def _():
            for way in (0, 1):
                r_copy(way, u, hops - 1, own(way, u, hops - 1)).wait_recv()
            home(u)

        return carry

    lax.fori_loop(0, units + hops, scatter, 0)
    zr_copy(1, 0).wait_recv()
    out = hidden[...] + recv_z[1, 0].astype(f32)
    layer_out[...] = out.astype(bf16)
    message = jnp.where(lane == 0, lane_sum(out * out), 0.0)
    message = jnp.where(lane == 1, lane_sum(out * value_gain[...]), message)
    total = both(1, message)
    estimate = total[:, 1:2] * lax.rsqrt(total[:, 0:1] / full_width + eps) + value_bias[0]
    values[...] = jnp.broadcast_to(jnp.where(my_pos < limit, estimate, 0.0), (count, META))

    def drain(u, carry):
        @pl.when(u > 0)
        def _():
            zr_copy(0, u).wait_send()

        zr_copy(1, u).wait_send()
        for way in (0, 1):

            @pl.when(lax.rem(u, 2) == way)
            def _():
                r_copy(way, u, 0, own(way, u, 0)).wait_send()

            for k in range(1, hops):
                r_copy(way, u, k, own(way, u, k)).wait_send()
        return carry

    lax.fori_loop(0, units, drain, 0)


def on_device(dims, *args):
    (stream, queries, key_rows, value_rows, routes, seq_length, norm_gain, router) = args[:8]
    (w_up, w_down, final_gain, value_weight, value_bias) = args[8:]
    nz, nx, _ = dims
    units, hops = nz // 2, nx // 2
    count, width = stream.shape
    hid = w_up.shape[1]
    vmem, smem, far = (
        pl.BlockSpec(memory_space=pltpu.VMEM),
        pl.BlockSpec(memory_space=pltpu.SMEM),
        pl.BlockSpec(memory_space=pl.ANY),
    )
    dma = pltpu.SemaphoreType.DMA
    layer_out, values = pl.pallas_call(
        functools.partial(kernel, dims),
        out_shape=(
            jax.ShapeDtypeStruct((count, width), bf16),
            jax.ShapeDtypeStruct((count, META), f32),
        ),
        in_specs=[vmem, far, far, vmem, vmem, smem, vmem, vmem, far, far, vmem, smem],
        out_specs=(vmem, vmem),
        scratch_shapes=[
            pltpu.VMEM((units, nx, 2, count, 2 * key_rows.shape[1]), bf16),
            pltpu.VMEM((units, 2, count, width + META), bf16),
            pltpu.VMEM((units, nx, count, width), bf16),
            pltpu.VMEM((count, width), f32),
            pltpu.VMEM(w_up.shape, bf16),
            pltpu.VMEM(w_down.shape, bf16),
            pltpu.VMEM((2, count, META), f32),
            pltpu.VMEM((2, count, META), f32),
            pltpu.VMEM((units, nx * count, hid), f32),
            pltpu.VMEM((units, nx * count, hid), f32),
            pltpu.VMEM((units, nx * count, hid), bf16),
            pltpu.VMEM((units, nx, count, width), bf16),
            pltpu.VMEM((units, hops, count, width), bf16),
            pltpu.VMEM((units, hops, count, width), bf16),
            pltpu.VMEM((units, hops, count, width), bf16),
            pltpu.VMEM((units, hops, count, width), bf16),
            pltpu.VMEM((2, units, count, width), bf16),
            pltpu.VMEM((2, units, count, width), bf16),
            dma((4,)),
            dma((2, units)),
            dma((2, units, hops)),
            dma((3, 2, units)),
            dma((3, 2, units, hops)),
            dma((2,)),
            dma((2,)),
            dma((units,)),
            dma((units,)),
        ],
        compiler_params=pltpu.CompilerParams(
            collective_id=0, has_side_effects=True, vmem_limit_bytes=56 * 2**20
        ),
        name="layer",
    )(
        queries,
        key_rows,
        value_rows,
        stream,
        routes,
        seq_length,
        norm_gain.reshape(1, width),
        router,
        w_up,
        w_down,
        (final_gain * value_weight).reshape(1, width),
        value_bias,
    )
    return layer_out, values[:, 0]


def build(mesh, nz, nx, full_width):
    finer = Mesh(
        mesh.devices.reshape(mesh.shape["groups"], nz, nx, mesh.shape["tp"]),
        ("groups", "z", "x", "tp"),
    )
    placed = (
        P(GROUPS_SEQ, "tp"),
        P(GROUPS_SEQ, "tp"),
        P(GROUPS_SEQ, "tp"),
        P(GROUPS_SEQ, "tp"),
        P(GROUPS_SEQ, None),
        P("groups"),
        P("tp"),
        P("tp", None),
        P("tp", SEQ),
        P(SEQ, "tp"),
        P("tp"),
        P("tp"),
        P(),
    )
    return jax.shard_map(
        functools.partial(on_device, (nz, nx, full_width)),
        mesh=finer,
        in_specs=placed,
        out_specs=(P(GROUPS_SEQ, "tp"), P(GROUPS_SEQ)),
        check_vma=False,
    )


def solution(mesh):
    return build(mesh, 16, mesh.shape["seq"] // 16, 6144)
```

time: 553 us -> 194 us (0.35)
  waiting for transfers between devices: 399 us -> 0 us
  Pallas kernels: 0 us -> 184 us
  blocking collectives: 75.5 us -> 0 us
  starting transfers between devices: 17.1 us -> 0 us
  matrix products: 15.9 us -> 0 us
  local copies, waits for them, and re-layouts: 21.4 us -> 6.52 us
  between operations: 16.3 us -> 1.93 us
  other arithmetic: 7.87 us -> 1.33 us
    all_gather x2 -> x0, waiting for transfers between devices: 266 us -> none  [the longest x1 170 us: sent_together(): result, at, done = (lax.all_gather(both, axis, axis=dim, tiled=True), 0, [])]
    pallas_call x0 -> x1, Pallas kernels: none -> 184 us  [on_device(): pl.pallas_call(functools.partial(kernel, dims), out_shape=(jax.ShapeDtype...]
    all_to_all x1 -> x0, waiting for transfers between devices: 133 us -> none  [on_device(): lax.all_to_all(partial_out, SEQ, split_axis=0, concat_axis=0, tiled=True)]
    all_gather x3 -> x0, blocking collectives: 42.8 us -> none  [the longest x2 40.7 us: stacked_from(): pieces = lax.all_gather(pieces, axes[k])]
    unnamed x2 -> x0, blocking collectives: 20.7 us -> none
    all_to_all x1 -> x0, starting transfers between devices: 17 us -> none  [on_device(): lax.all_to_all(partial_out, SEQ, split_axis=0, concat_axis=0, tiled=True)]
    dot_general x7 -> x0, matrix products: 15.9 us -> none  [the longest x1 6.26 us: on_device(): jnp.einsum('src,srd->scd', selector, every_row.reshape(seq_devices, row_c...]
    reshape x3 -> x0, local copies, waits for them, and re-layouts: 12 us -> none  [the longest x1 6.11 us: on_device(): partial_out = down_part.reshape(lead, items, half_width)]
  transfers between devices with their start and end apart: 3 -> 0, of which waited for: 3 -> 0; matrix products, arithmetic and copies ran while one was open for 1% -> 0% of each run, Pallas kernels for 0% -> 0%
where the time goes in v1:
time: 194 us; the launch traced here: 193 us
  Pallas kernels  184 us (95%)
  local copies, waits for them, and re-layouts  6.52 us (3%)
    pallas_call x1, Pallas kernels, on_device(): pl.pallas_call(functools.partial(kernel, dims), out_shape=(jax.ShapeDtype...  184 us
    unnamed x3, local copies, waits for them, and re-layouts  5.22 us

profile of v1, /device:TPU:65, one launch (start us, length us, event | category | flops | bytes accessed | tf_op | source)
XLA Modules:
  0.0 193.4 jit_solution(4753087506537341126)
XLA Ops:
  1.9 1.3 copy.17.routes
  3.3 1.3 mul.3
  4.6 2.5 %copy.18.router = f32[3072,4]{1,0:T(8,128)} copy(f32[3072,4]{0,1:T(4,128)} %param.20) | data formatting | bytes 98304 | tf_op args[7]
  7.1 183.6 %layer.1 = (bf16[8,3072]{1,0:T(8,128)(2,1)}, f32[8,128]{1,0:T(8,128)}) custom-call(bf16[8,3072]{1,0:T(8,128)(2,1)} %queries.1, bf16[8,512]{1,0:T(8,128)(2,1)} %key_rows.1, bf16[8,512]{1,0:T(8,128)(2,1)} %value_rows.1, bf16[8,3072]{1,0:T(8,128)(2,1)} %stream.1, s32[8,2]{1,0:T(8,128)} %copy.17.routes, s32[1]{0:T(128)S(6)} %copy.20.seq_length, ...), custom_call_target="tpu_custom_call" | custom-call | tf_op jit(solution)/shard_map/layer/pallas_call | solution.py:470
  190.6 1.3 slice_reduce_fusion
  191.9 1.4 copy.22

commit v2 on v1

v2 whole, which is shorter than its diff:
```python
import functools
import math

import jax
import jax.numpy as jnp
from jax import lax
from jax.experimental import pallas as pl
from jax.experimental.pallas import tpu as pltpu
from jax.sharding import Mesh
from jax.sharding import PartitionSpec as P

HD = 128
EXPERTS = 4
META = 128
SEQ = ("z", "x")
GROUPS_SEQ = ("groups", "z", "x")
eps = 1e-05
masked = -1e30
f32 = jnp.float32
bf16 = jnp.bfloat16


def lane_sum(a):
    return jnp.sum(a, axis=1, keepdims=True)


def kernel(
    dims,
    queries,
    key_rows,
    value_rows,
    stream,
    routes,
    seq_length,
    norm_gain,
    router,
    w_up_hbm,
    w_down_hbm,
    final_gain,
    value_weight,
    value_bias,
    layer_out,
    values,
    q_all,
    kv_own,
    kv,
    att_out,
    att_in,
    top_score,
    weight_sum,
    mixed_values,
    rows_z,
    rows_x,
    hidden,
    info,
    w_up,
    w_down,
    stats,
    stats_in,
    ups,
    ups_in,
    parts,
    sums,
    recv,
    back_out,
    back_in,
    local_sem,
    asend,
    arecv,
    zsend,
    zrecv,
    xsend,
    xrecv,
    bsend,
    brecv,
    tsend,
    trecv,
    usend,
    urecv,
):
    nz, nx, full_width = dims
    units, hops = nz // 2, nx // 2
    z, x, t = lax.axis_index("z"), lax.axis_index("x"), lax.axis_index("tp")
    right, left = {"x": lax.rem(x + 1, nx)}, {"x": lax.rem(x + nx - 1, nx)}
    twin = {"tp": 1 - t}
    count, width = stream.shape
    kv_width = key_rows.shape[1]
    q_width = width // nx
    sharers = nx // (kv_width // HD)

    def along_z(steps):
        return {"z": lax.rem(z + nz + steps, nz)}

    def remote(src, dst, send, recv, to):
        return pltpu.make_async_remote_copy(
            src_ref=src, dst_ref=dst, send_sem=send, recv_sem=recv, device_id=to,
            device_id_type=pl.DeviceIdType.MESH,
        )

    up_copy = pltpu.make_async_copy(w_up_hbm, w_up, local_sem.at[0])
    down_copy = pltpu.make_async_copy(w_down_hbm, w_down, local_sem.at[1])
    up_copy.start()
    down_copy.start()
    barrier = pltpu.get_barrier_semaphore()

    def greet(peer):
        pl.semaphore_signal(barrier, inc=1, device_id=peer, device_id_type=pl.DeviceIdType.MESH)

    for steps in (1, -1, 2, -2):
        greet(along_z(steps))
    for d in range(1, nx):
        greet({"x": lax.rem(x + d, nx)})
    greet(twin)
    for head in range(kv_width // HD):
        kv_own[head, :, :HD] = key_rows[:, head * HD : (head + 1) * HD]
        kv_own[head, :, HD:] = value_rows[:, head * HD : (head + 1) * HD]
    kv[0, 0, x] = kv_own[x // sharers]
    q_all[x] = queries[:, pl.ds(pl.multiple_of(x * q_width, HD), q_width)]
    pl.semaphore_wait(barrier, 4 + nx)

    def q_copy(d):
        peer = lax.rem(x + d, nx)
        at = pl.ds(pl.multiple_of(peer * q_width, HD), q_width)
        return remote(queries.at[:, at], q_all.at[x], asend.at[0, d], arecv.at[0, d], {"x": peer})

    def kv_copy(d):
        peer = lax.rem(x + d, nx)
        return remote(kv_own.at[peer // sharers], kv.at[0, 0, x], asend.at[1, d], arecv.at[1, d], {"x": peer})

    def att_copy(d):
        peer = lax.rem(x + d, nx)
        return remote(att_out.at[peer], att_in.at[x], asend.at[2, d], arecv.at[2, d], {"x": peer})

    far_first = sorted(range(1, nx), key=lambda d: -min(d, nx - d))
    for d in far_first:
        kv_copy(d).start()
    for d in far_first:
        q_copy(d).start()

    def z_ring(phase, at):
        def first(way, u):
            steps = (-u if u < 3 else -2) if way == 0 else min(u + 1, 2)
            src = at(0, 0) if (u < 3 and way == 0) or u < 2 else at(u - 2, way)
            return remote(src, at(u, way), zsend.at[way, u], zrecv.at[phase, way, u], along_z(steps))

        def onward(way, u):
            return remote(
                at(u - 2, way), at(u, way), zsend.at[way, u], zrecv.at[phase, way, u],
                along_z(-2 if way == 0 else 2),
            )

        def start():
            for way, u in ((0, 2), (1, 1), (0, 1), (1, 0)):
                first(way, u).start()

        def take(u):
            @pl.when(u > 0)
            def _():
                onward(0, u).wait_recv()

                @pl.when(u + 2 < units)
                def _():
                    onward(0, u + 2).start()

            onward(1, u).wait_recv()

            @pl.when(u + 2 < units)
            def _():
                onward(1, u + 2).start()

        def drain(u):
            @pl.when(u > 0)
            def _():
                onward(0, u).wait_send()

            onward(1, u).wait_send()

        return start, take, drain

    kv_start, kv_take, kv_drain = z_ring(0, lambda u, half: kv.at[lax.max(u, 0), half])
    for d in range(1, nx):
        kv_copy(d).wait_recv()
    kv_start()
    for d in range(1, nx):
        q_copy(d).wait_recv()

    mine = nx * count
    per = q_width // HD
    limit = seq_length[0]
    top_score[...] = jnp.full(top_score.shape, masked, f32)
    weight_sum[...] = jnp.zeros(weight_sum.shape, f32)
    mixed_values[...] = jnp.zeros(mixed_values.shape, f32)
    q_row = lax.broadcasted_iota(jnp.int32, (per * mine, 2 * mine), 0)
    k_row = lax.broadcasted_iota(jnp.int32, (per * mine, 2 * mine), 1)
    q_pos = z * mine + lax.rem(q_row, mine)

    def attend(u, carry):
        kv_take(u)
        q = jnp.concatenate(
            [q_all[:, :, j * HD : (j + 1) * HD].reshape(mine, HD) for j in range(per)], axis=0
        )
        k = kv[u, :, :, :, :HD].reshape(2 * mine, HD)
        v = kv[u, :, :, :, HD:].reshape(2 * mine, HD)
        s = lax.dot_general(q, k, (((1,), (1,)), ((), ())), preferred_element_type=f32) * (1.0 / math.sqrt(HD))
        k_pos = jnp.where(
            k_row < mine, lax.rem(z + u, nz) * mine + k_row, lax.rem(z - u - 1 + nz, nz) * mine + k_row - mine
        )
        allowed = (k_pos <= q_pos) & (k_pos < limit)
        s = jnp.where(allowed, s, masked)
        old = top_score[:, 0:1]
        new = jnp.maximum(old, jnp.max(s, axis=1, keepdims=True))
        p = jnp.where(allowed, jnp.exp(s - new), 0.0)
        keep = jnp.exp(old - new)
        top_score[...] = jnp.broadcast_to(new, top_score.shape)
        weight_sum[...] = weight_sum[...] * keep + lane_sum(p)
        mixed_values[...] = mixed_values[...] * keep + jnp.dot(p.astype(bf16), v, preferred_element_type=f32)
        return carry

    lax.fori_loop(0, units, attend, 0)
    attended = mixed_values[...] / weight_sum[...]
    for s in range(nx):
        for j in range(per):
            piece = attended[j * mine + s * count : j * mine + (s + 1) * count]
            att_out[s, :, j * HD : (j + 1) * HD] = piece.astype(bf16)
    att_in[x] = att_out[x]
    for d in far_first:
        att_copy(d).start()
    for d in range(1, nz):
        greet(along_z(d))

    def kv_sent(u, carry):
        kv_drain(u)
        return carry

    lax.fori_loop(0, units, kv_sent, 0)
    for d in range(1, nx):
        kv_copy(d).wait_send()
        q_copy(d).wait_send()
    for d in range(1, nx):
        att_copy(d).wait_recv()
    for s in range(nx):
        at = slice(s * q_width, (s + 1) * q_width)
        hidden[:, at] = stream[:, at].astype(f32) + att_in[s].astype(f32)

    def both(index, message):
        stats[index] = message
        copy = remote(stats.at[index], stats_in.at[index], tsend.at[index], trecv.at[index], twin)
        copy.start()
        copy.wait()
        return message + stats_in[index]

    lane = lax.broadcasted_iota(jnp.int32, (count, META), 1)
    row = lax.broadcasted_iota(jnp.int32, (count, META), 0)

    def upright(line):
        return lane_sum(jnp.where(lane == row, jnp.broadcast_to(line, (count, META)), 0.0))

    h_all = hidden[...]
    gained = h_all * norm_gain[...]
    message = jnp.where(lane == EXPERTS, lane_sum(h_all * h_all), 0.0)
    for e in range(EXPERTS):
        message = jnp.where(lane == e, lane_sum(gained * router[e : e + 1]), message)
    total = both(0, message)
    sq = lane_sum(jnp.where(lane == EXPERTS, total, 0.0))
    scale = lax.rsqrt(sq / full_width + eps)
    logits = total * scale
    spread = jnp.concatenate([routes[...].astype(f32), jnp.zeros((2, META - count), f32)], axis=1)
    first, second = upright(spread[0:1]).astype(jnp.int32), upright(spread[1:2]).astype(jnp.int32)
    hit_a, hit_b = lane == first, lane == second
    gap = lane_sum(jnp.where(hit_a, logits, 0.0)) - lane_sum(jnp.where(hit_b, logits, 0.0))
    gate_a, gate_b = 1.0 / (1.0 + jnp.exp(-gap)), 1.0 / (1.0 + jnp.exp(gap))
    hits = jnp.where(hit_a | hit_b, 1.0, 0.0)
    rank = jnp.zeros((count, META), f32)
    for i in range(count - 1):
        rank = rank + jnp.where(row > i, jnp.broadcast_to(hits[i : i + 1], (count, META)), 0.0)
    place = jnp.where(hits > 0.5, rank + 1.0, 0.0)
    rows_z[0, 0, :, :width] = (gained * scale).astype(bf16)
    rows_z[0, 0, :, width:] = place.astype(bf16)
    rows_start, rows_take, rows_drain = z_ring(1, lambda u, half: rows_z.at[lax.max(u, 0), half])
    rows_start()
    info[0] = place
    info[1] = jnp.where(hit_a, gate_a, jnp.where(hit_b, gate_b, 0.0))

    my_expert = z // (nz // EXPERTS)
    slots = count // 2

    def column(table, expert):
        return lane_sum(jnp.where(lane == expert, table, 0.0))

    def choose(u):
        out = jnp.zeros((count, width), f32)
        for half in (0, 1):
            block = rows_z[u, half].astype(f32)
            places = jnp.broadcast_to(column(block[:, width:], my_expert), (count, META))
            for i in range(count):
                want = jnp.broadcast_to(places[i : i + 1], (count, META)) + (slots * half)
                chosen = jnp.where(((row + 1).astype(f32) == want) & (want > slots * half + 0.5), 1.0, 0.0)
                out = out + chosen[:, 0:1] * block[i : i + 1, :width]
        rows_x[u, x] = out.astype(bf16)

    def g_copy(way, u, h):
        back = nx - (h - 1) if way == 0 else h - 1
        at = rows_x.at[u, lax.rem(x + back, nx)]
        return remote(
            at, at, xsend.at[0, way, u, h - 1], xrecv.at[0, way, u, h - 1], right if way == 0 else left
        )

    def ups_copy(u):
        return remote(ups.at[u], ups_in.at[u], usend.at[u], urecv.at[u], twin)

    def project(u):
        ups[u] = jnp.dot(rows_x[u].reshape(mine, width), w_up[...], preferred_element_type=f32)
        ups_copy(u).start()

    def own(way, u, k):
        ahead = hops - k
        return parts.at[u, lax.rem(x + (ahead if way == 0 else nx - ahead), nx)]

    def r_copy(way, u, k, src):
        return remote(
            src, recv.at[way, u, k], xsend.at[1, way, u, k], xrecv.at[1, way, u, k], right if way == 0 else left
        )

    def expand(u):
        ups_copy(u).wait_recv()
        v = ups[u] + ups_in[u]
        active = (v / (1.0 + jnp.exp(-v))).astype(bf16)
        made = jnp.dot(active, w_down[...], preferred_element_type=f32)
        for d in range(nx):
            parts[u, d] = made[d * count : (d + 1) * count].astype(bf16)
        for way in (0, 1):

            @pl.when(lax.rem(u, 2) == way)
            def _():
                r_copy(way, u, 0, own(way, u, 0)).start()

    def back_copy(half, u):
        steps = u if half == 0 else -u - 1
        return remote(back_out.at[u, half], back_in.at[u, half], bsend.at[half, u], brecv.at[half, u], along_z(steps))

    def home(u):
        for way in (0, 1):
            r_copy(way, u, hops - 1, own(way, u, hops - 1)).wait_recv()
        both_ways = recv[0, u, hops - 1].astype(f32) + recv[1, u, hops - 1].astype(f32)
        done = (parts[u, x].astype(f32) + both_ways).astype(bf16)

        @pl.when(u > 0)
        def _():
            back_out[u, 0] = done[:slots]
            back_copy(0, u).start()

        @pl.when(u == 0)
        def _():
            back_in[0, 0] = done[:slots]

        back_out[u, 1] = done[slots:]
        back_copy(1, u).start()

    def blend(u):
        @pl.when(u > 0)
        def _():
            back_copy(0, u).wait_recv()

        back_copy(1, u).wait_recv()
        mix = hidden[...]
        for half in (0, 1):
            source = lax.rem(z - u + nz, nz) if half == 0 else lax.rem(z + u + 1, nz)
            expert = source // (nz // EXPERTS)
            places, gate = column(info[0], expert), column(info[1], expert)
            got = back_in[u, half].astype(f32)
            for i in range(slots):
                mix = mix + jnp.where(places == float(i + 1), gate, 0.0) * got[i : i + 1]
        hidden[...] = mix

    for d in range(1, nx):
        att_copy(d).wait_send()
    up_copy.wait()
    down_copy.wait()
    pl.semaphore_wait(barrier, nz - 1)
    lag = hops + 1

    def slot(step, carry):
        @pl.when(step < units)
        def _():
            rows_take(step)
            choose(step)
            g_copy(0, step, 1).start()
            g_copy(1, step, 1).start()

        for h in range(1, hops):
            u = step - h

            @pl.when((u >= 0) & (u < units))
            def _():
                for way in (0, 1):
                    g_copy(way, u, h).wait_recv()
                    if h < hops - 1:
                        g_copy(way, u, h + 1).start()
                    else:

                        @pl.when(lax.rem(u, 2) == way)
                        def _():
                            g_copy(way, u, h + 1).start()

        for k in range(1, hops):
            u = step - lag - k

            @pl.when((u >= 0) & (u < units))
            def _():
                for way in (0, 1):

                    def add():
                        r_copy(way, u, k - 1, own(way, u, k - 1)).wait_recv()
                        total = recv[way, u, k - 1].astype(f32) + own(way, u, k)[...].astype(f32)
                        sums[way, u, k] = total.astype(bf16)
                        r_copy(way, u, k, sums.at[way, u, k]).start()

                    if k > 1:
                        add()
                    else:
                        pl.when(lax.rem(u, 2) == way)(add)

                        @pl.when(lax.rem(u, 2) != way)
                        def _():
                            r_copy(way, u, k, own(way, u, k)).start()

        u_in = step - hops

        @pl.when((u_in >= 0) & (u_in < units))
        def _():
            for way in (0, 1):

                @pl.when(lax.rem(u_in, 2) == way)
                def _():
                    g_copy(way, u_in, hops).wait_recv()

            project(u_in)

        u_mid = step - lag

        @pl.when((u_mid >= 0) & (u_mid < units))
        def _():
            expand(u_mid)

        u_out = step - lag - hops

        @pl.when((u_out >= 0) & (u_out < units))
        def _():
            home(u_out)

        u_last = step - lag - hops - 2

        @pl.when(u_last >= 0)
        def _():
            blend(u_last)

        return carry

    lax.fori_loop(0, units + lag + hops + 2, slot, 0)
    out = hidden[...]
    layer_out[...] = out.astype(bf16)
    message = jnp.where(lane == 0, lane_sum(out * out), 0.0)
    message = jnp.where(lane == 1, lane_sum(out * (final_gain[...] * value_weight[...])), message)
    total = both(1, message)
    estimate = total[:, 1:2] * lax.rsqrt(total[:, 0:1] / full_width + eps) + value_bias[0]
    real = (z * nx + x) * count + row < limit
    flat = jnp.sum(jnp.where((lane == row) & real, estimate, 0.0), axis=0, keepdims=True)
    values[...] = flat

    def drain(u, carry):
        rows_drain(u)
        ups_copy(u).wait_send()

        @pl.when(u > 0)
        def _():
            back_copy(0, u).wait_send()

        back_copy(1, u).wait_send()
        for way in (0, 1):
            for k in range(1, hops):
                g_copy(way, u, k).wait_send()
                r_copy(way, u, k, own(way, u, k)).wait_send()

            @pl.when(lax.rem(u, 2) == way)
            def _():
                g_copy(way, u, hops).wait_send()
                r_copy(way, u, 0, own(way, u, 0)).wait_send()

        return carry

    lax.fori_loop(0, units, drain, 0)


def on_device(dims, *args):
    (stream, queries, key_rows, value_rows, routes, seq_length, norm_gain, router) = args[:8]
    (w_up, w_down, final_gain, value_weight, value_bias) = args[8:]
    nz, nx, _ = dims
    units, hops = nz // 2, nx // 2
    count, width = stream.shape
    hid = w_up.shape[1]
    heads = key_rows.shape[1] // HD
    mine = nx * count
    stacked = width // nx // HD * mine
    vmem, smem, far = (
        pl.BlockSpec(memory_space=pltpu.VMEM),
        pl.BlockSpec(memory_space=pltpu.SMEM),
        pl.BlockSpec(memory_space=pl.ANY),
    )
    dma = pltpu.SemaphoreType.DMA
    layer_out, values = pl.pallas_call(
        functools.partial(kernel, dims),
        out_shape=(
            jax.ShapeDtypeStruct((count, width), bf16),
            jax.ShapeDtypeStruct((1, META), f32),
        ),
        in_specs=[vmem, vmem, vmem, vmem, vmem, smem, vmem, vmem, far, far, vmem, vmem, smem],
        out_specs=(vmem, vmem),
        scratch_shapes=[
            pltpu.VMEM((nx, count, width // nx), bf16),
            pltpu.VMEM((heads, count, 2 * HD), bf16),
            pltpu.VMEM((units, 2, nx, count, 2 * HD), bf16),
            pltpu.VMEM((nx, count, width // nx), bf16),
            pltpu.VMEM((nx, count, width // nx), bf16),
            pltpu.VMEM((stacked, HD), f32),
            pltpu.VMEM((stacked, HD), f32),
            pltpu.VMEM((stacked, HD), f32),
            pltpu.VMEM((units, 2, count, width + META), bf16),
            pltpu.VMEM((units, nx, count, width), bf16),
            pltpu.VMEM((count, width), f32),
            pltpu.VMEM((2, count, META), f32),
            pltpu.VMEM(w_up.shape, bf16),
            pltpu.VMEM(w_down.shape, bf16),
            pltpu.VMEM((2, count, META), f32),
            pltpu.VMEM((2, count, META), f32),
            pltpu.VMEM((units, mine, hid), f32),
            pltpu.VMEM((units, mine, hid), f32),
            pltpu.VMEM((units, nx, count, width), bf16),
            pltpu.VMEM((2, units, hops, count, width), bf16),
            pltpu.VMEM((2, units, hops, count, width), bf16),
            pltpu.VMEM((units, 2, count // 2, width), bf16),
            pltpu.VMEM((units, 2, count // 2, width), bf16),
            dma((2,)),
            dma((3, nx)),
            dma((3, nx)),
            dma((2, units)),
            dma((2, 2, units)),
            dma((2, 2, units, hops)),
            dma((2, 2, units, hops)),
            dma((2, units)),
            dma((2, units)),
            dma((2,)),
            dma((2,)),
            dma((units,)),
            dma((units,)),
        ],
        compiler_params=pltpu.CompilerParams(
            collective_id=0, has_side_effects=True, vmem_limit_bytes=56 * 2**20
        ),
        name="layer",
    )(
        queries,
        key_rows,
        value_rows,
        stream,
        routes.T,
        seq_length,
        norm_gain.reshape(1, width),
        router.T,
        w_up,
        w_down,
        final_gain.reshape(1, width),
        value_weight.reshape(1, width),
        value_bias,
    )
    return layer_out, values[0, :count]


def build(mesh, nz, nx, full_width):
    finer = Mesh(
        mesh.devices.reshape(mesh.shape["groups"], nz, nx, mesh.shape["tp"]),
        ("groups", "z", "x", "tp"),
    )
    placed = (
        P(GROUPS_SEQ, "tp"),
        P(GROUPS_SEQ, "tp"),
        P(GROUPS_SEQ, "tp"),
        P(GROUPS_SEQ, "tp"),
        P(GROUPS_SEQ, None),
        P("groups"),
        P("tp"),
        P("tp", None),
        P("tp", SEQ),
        P(SEQ, "tp"),
        P("tp"),
        P("tp"),
        P(),
    )
    return jax.shard_map(
        functools.partial(on_device, (nz, nx, full_width)),
        mesh=finer,
        in_specs=placed,
        out_specs=(P(GROUPS_SEQ, "tp"), P(GROUPS_SEQ)),
        check_vma=False,
    )


def solution(mesh):
    return build(mesh, 16, mesh.shape["seq"] // 16, 6144)
```

time: 194 us -> 176 us (0.907)
  Pallas kernels: 184 us -> 171 us
  local copies, waits for them, and re-layouts: 6.52 us -> 2.57 us
    pallas_call x1, Pallas kernels: 184 us -> 171 us  [on_device(): pl.pallas_call(functools.partial(kernel, dims), out_shape=(jax.ShapeDtype...]
    unnamed x3 -> x1, local copies, waits for them, and re-layouts: 5.22 us -> 1.42 us
where the time goes in v2:
time: 176 us
  Pallas kernels  171 us (97%)
  local copies, waits for them, and re-layouts  2.57 us (1%)
  between operations  1.93 us (1%)
    pallas_call x1, Pallas kernels, on_device(): pl.pallas_call(functools.partial(kernel, dims), out_shape=(jax.ShapeDtype...  171 us

profile of v2, /device:TPU:65, one launch (start us, length us, event | category | flops | bytes accessed | tf_op | source)
XLA Modules:
  0.0 176.0 jit_solution(7104022754537807793)
XLA Ops:
  1.9 171.5 %layer.1 = (bf16[8,3072]{1,0:T(8,128)(2,1)}, f32[1,128]{1,0:T(1,128)}) custom-call(bf16[8,3072]{1,0:T(8,128)(2,1)} %queries.1, bf16[8,512]{1,0:T(8,128)(2,1)} %key_rows.1, bf16[8,512]{1,0:T(8,128)(2,1)} %value_rows.1, bf16[8,3072]{1,0:T(8,128)(2,1)} %stream.1, s32[2,8]{1,0:T(2,128)} %bitcast.11, s32[1]{0:T(128)S(6)} %copy.16.seq_length, f32[1,3072]{1,0:T(1,128)} %bitcast.8, ...), custom_call_target="tpu_custom_call" | custom-call | tf_op jit(solution)/shard_map/layer/pallas_call | solution.py:510
  173.4 1.1 slice_bitcast_fusion
  174.5 1.4 copy.18

commit v3 on v2

--- a/solution.py
+++ b/solution.py
@@ -16,6 +16,7 @@
 GROUPS_SEQ = ("groups", "z", "x")
 eps = 1e-05
 masked = -1e30
+chunks = 4
 f32 = jnp.float32
 bf16 = jnp.bfloat16
 
@@ -49,16 +50,24 @@
     top_score,
     weight_sum,
     mixed_values,
+    rows_out,
     rows_z,
     rows_x,
     hidden,
     info,
     w_up,
     w_down,
+    w_up_in,
+    w_down_in,
     stats,
     stats_in,
     ups,
+    ups_out,
     ups_in,
+    ups_half,
+    ups_twin,
+    act_out,
+    act_in,
     parts,
     sums,
     recv,
@@ -77,6 +86,8 @@
     trecv,
     usend,
     urecv,
+    wsend,
+    wrecv,
 ):
     nz, nx, full_width = dims
     units, hops = nz // 2, nx // 2
@@ -97,8 +108,26 @@
             device_id_type=pl.DeviceIdType.MESH,
         )
 
-    up_copy = pltpu.make_async_copy(w_up_hbm, w_up, local_sem.at[0])
-    down_copy = pltpu.make_async_copy(w_down_hbm, w_down, local_sem.at[1])
+    c = lax.rem(z, 2)
+    m, pairs = z // 2, nz // 2
+    narrow, hid = width // 2, w_up_hbm.shape[1]
+    mate = {"z": z + 1 - 2 * c}
+    keep_cols = pl.ds(pl.multiple_of(c * narrow, HD), narrow)
+    give_cols = pl.ds(pl.multiple_of((1 - c) * narrow, HD), narrow)
+    up_copy = pltpu.make_async_copy(w_up_hbm.at[keep_cols, :], w_up, local_sem.at[0])
+    down_copy = pltpu.make_async_copy(w_down_hbm.at[:, keep_cols], w_down, local_sem.at[1])
+
+    def weight_copy(k):
+        if k < chunks:
+            size = narrow // chunks
+            at = pl.ds(pl.multiple_of((1 - c) * narrow + k * size, HD // 2), size)
+            return remote(
+                w_up_hbm.at[at, :], w_up_in.at[pl.ds(k * size, size), :], wsend.at[k], wrecv.at[k], mate
+            )
+        size = hid // chunks
+        at = pl.ds((k - chunks) * size, size)
+        return remote(w_down_hbm.at[at, give_cols], w_down_in.at[at, :], wsend.at[k], wrecv.at[k], mate)
+
     up_copy.start()
     down_copy.start()
     barrier = pltpu.get_barrier_semaphore()
@@ -216,7 +245,11 @@
         mixed_values[...] = mixed_values[...] * keep + jnp.dot(p.astype(bf16), v, preferred_element_type=f32)
         return carry
 
-    lax.fori_loop(0, units, attend, 0)
+    each = 2 * chunks // units
+    for u in range(units):
+        attend(u, 0)
+        for k in range(u * each, (u + 1) * each):
+            weight_copy(k).start()
     attended = mixed_values[...] / weight_sum[...]
     for s in range(nx):
         for j in range(per):
@@ -274,10 +307,51 @@
     for i in range(count - 1):
         rank = rank + jnp.where(row > i, jnp.broadcast_to(hits[i : i + 1], (count, META)), 0.0)
     place = jnp.where(hits > 0.5, rank + 1.0, 0.0)
-    rows_z[0, 0, :, :width] = (gained * scale).astype(bf16)
-    rows_z[0, 0, :, width:] = place.astype(bf16)
-    rows_start, rows_take, rows_drain = z_ring(1, lambda u, half: rows_z.at[lax.max(u, 0), half])
-    rows_start()
+    normed = gained * scale
+    low, high = normed[:, :narrow], normed[:, narrow:]
+    rows_out[:, :narrow] = jnp.where(c == 0, high, low).astype(bf16)
+    rows_out[:, narrow:] = place.astype(bf16)
+    rows_z[0, c, :, :narrow] = jnp.where(c == 0, low, high).astype(bf16)
+    rows_z[0, c, :, narrow:] = place.astype(bf16)
+
+    def mate_rows():
+        return remote(rows_out, rows_z.at[0, c], zsend.at[0, 0], zrecv.at[1, 0, 0], mate)
+
+    def rows_copy(b, u):
+        return remote(
+            rows_z.at[lax.max(u - 2, 0), b], rows_z.at[u, b], zsend.at[b, u], zrecv.at[1, b, u],
+            along_z(2 - 4 * lax.rem(u, 2)),
+        )
+
+    mate_rows().start()
+
+    def rows_take(u):
+        @pl.when(u == 0)
+        def _():
+            mate_rows().wait_recv()
+            for b in (0, 1):
+                rows_copy(b, 1).start()
+                rows_copy(b, 2).start()
+
+        @pl.when(u > 0)
+        def _():
+            for b in (0, 1):
+                rows_copy(b, u).wait_recv()
+
+                @pl.when(u + 2 < units)
+                def _():
+                    rows_copy(b, u + 2).start()
+
+    def rows_drain(u):
+        @pl.when(u == 0)
+        def _():
+            mate_rows().wait_send()
+
+        @pl.when(u > 0)
+        def _():
+            for b in (0, 1):
+                rows_copy(b, u).wait_send()
+
     info[0] = place
     info[1] = jnp.where(hit_a, gate_a, jnp.where(hit_b, gate_b, 0.0))
 
@@ -288,14 +362,14 @@
         return lane_sum(jnp.where(lane == expert, table, 0.0))
 
     def choose(u):
-        out = jnp.zeros((count, width), f32)
+        out = jnp.zeros((count, narrow), f32)
         for half in (0, 1):
             block = rows_z[u, half].astype(f32)
-            places = jnp.broadcast_to(column(block[:, width:], my_expert), (count, META))
+            places = jnp.broadcast_to(column(block[:, narrow:], my_expert), (count, META))
             for i in range(count):
                 want = jnp.broadcast_to(places[i : i + 1], (count, META)) + (slots * half)
                 chosen = jnp.where(((row + 1).astype(f32) == want) & (want > slots * half + 0.5), 1.0, 0.0)
-                out = out + chosen[:, 0:1] * block[i : i + 1, :width]
+                out = out + chosen[:, 0:1] * block[i : i + 1, :narrow]
         rows_x[u, x] = out.astype(bf16)
 
     def g_copy(way, u, h):
@@ -306,11 +380,30 @@
         )
 
     def ups_copy(u):
-        return remote(ups.at[u], ups_in.at[u], usend.at[u], urecv.at[u], twin)
+        return remote(ups_out.at[u], ups_in.at[u], usend.at[0, u], urecv.at[0, u], mate)
+
+    def twin_copy(u):
+        return remote(ups_half.at[u], ups_twin.at[u], usend.at[1, u], urecv.at[1, u], twin)
+
+    def act_copy(u):
+        return remote(act_out.at[u], act_in.at[u], usend.at[2, u], urecv.at[2, u], mate)
 
     def project(u):
-        ups[u] = jnp.dot(rows_x[u].reshape(mine, width), w_up[...], preferred_element_type=f32)
+        got = rows_x[u].reshape(mine, narrow)
+        ups_out[u] = jnp.dot(got, w_up_in[...], preferred_element_type=f32).astype(bf16)
         ups_copy(u).start()
+        ups[u] = jnp.dot(got, w_up[...], preferred_element_type=f32)
+
+    def merge(u):
+        ups_copy(u).wait_recv()
+        ups_half[u] = ups[u] + ups_in[u].astype(f32)
+        twin_copy(u).start()
+
+    def activate(u):
+        twin_copy(u).wait_recv()
+        v = ups_half[u] + ups_twin[u]
+        act_out[u] = (v / (1.0 + jnp.exp(-v))).astype(bf16)
+        act_copy(u).start()
 
     def own(way, u, k):
         ahead = hops - k
@@ -322,10 +415,9 @@
         )
 
     def expand(u):
-        ups_copy(u).wait_recv()
-        v = ups[u] + ups_in[u]
-        active = (v / (1.0 + jnp.exp(-v))).astype(bf16)
-        made = jnp.dot(active, w_down[...], preferred_element_type=f32)
+        act_copy(u).wait_recv()
+        made = jnp.dot(act_out[u], w_down[...], preferred_element_type=f32)
+        made = made + jnp.dot(act_in[u], w_down_in[...], preferred_element_type=f32)
         for d in range(nx):
             parts[u, d] = made[d * count : (d + 1) * count].astype(bf16)
         for way in (0, 1):
@@ -334,9 +426,16 @@
             def _():
                 r_copy(way, u, 0, own(way, u, 0)).start()
 
-    def back_copy(half, u):
-        steps = u if half == 0 else -u - 1
-        return remote(back_out.at[u, half], back_in.at[u, half], bsend.at[half, u], brecv.at[half, u], along_z(steps))
+    def offset(u):
+        return ((u + 1) // 2) * (2 * lax.rem(u, 2) - 1)
+
+    def back_copy(b, u):
+        to = {"z": 2 * lax.rem(m + offset(u) + pairs, pairs) + b}
+        return remote(back_out.at[u, b], back_in.at[u, c], bsend.at[b, u], brecv.at[c, u], to)
+
+    def back_arrival(b, u):
+        to = {"z": 2 * lax.rem(m + offset(u) + pairs, pairs) + b}
+        return remote(back_out.at[u, b], back_in.at[u, b], bsend.at[b, u], brecv.at[b, u], to)
 
     def home(u):
         for way in (0, 1):
@@ -344,40 +443,43 @@
         both_ways = recv[0, u, hops - 1].astype(f32) + recv[1, u, hops - 1].astype(f32)
         done = (parts[u, x].astype(f32) + both_ways).astype(bf16)
 
-        @pl.when(u > 0)
-        def _():
-            back_out[u, 0] = done[:slots]
-            back_copy(0, u).start()
-
-        @pl.when(u == 0)
-        def _():
-            back_in[0, 0] = done[:slots]
-
-        back_out[u, 1] = done[slots:]
-        back_copy(1, u).start()
+        for b in (0, 1):
+            back_out[u, b] = done[b * slots : (b + 1) * slots]
+
+            @pl.when((u > 0) | (c != b))
+            def _():
+                back_copy(b, u).start()
+
+            @pl.when((u == 0) & (c == b))
+            def _():
+                back_in[0, b] = done[b * slots : (b + 1) * slots]
 
     def blend(u):
-        @pl.when(u > 0)
-        def _():
-            back_copy(0, u).wait_recv()
-
-        back_copy(1, u).wait_recv()
-        mix = hidden[...]
-        for half in (0, 1):
-            source = lax.rem(z - u + nz, nz) if half == 0 else lax.rem(z + u + 1, nz)
-            expert = source // (nz // EXPERTS)
-            places, gate = column(info[0], expert), column(info[1], expert)
-            got = back_in[u, half].astype(f32)
+        source = lax.rem(m - offset(u) + pairs, pairs)
+        expert = 2 * source // (nz // EXPERTS)
+        places, gate = column(info[0], expert), column(info[1], expert)
+        weights = [jnp.where(places == float(i + 1), gate, 0.0) for i in range(slots)]
+        for b in (0, 1):
+
+            @pl.when((u > 0) | (c != b))
+            def _():
+                back_arrival(b, u).wait_recv()
+
+            at = slice(b * narrow, (b + 1) * narrow)
+            got = back_in[u, b].astype(f32)
+            mix = hidden[:, at]
             for i in range(slots):
-                mix = mix + jnp.where(places == float(i + 1), gate, 0.0) * got[i : i + 1]
-        hidden[...] = mix
+                mix = mix + weights[i] * got[i : i + 1]
+            hidden[:, at] = mix
 
     for d in range(1, nx):
         att_copy(d).wait_send()
     up_copy.wait()
     down_copy.wait()
     pl.semaphore_wait(barrier, nz - 1)
-    lag = hops + 1
+    for k in range(2 * chunks):
+        weight_copy(k).wait_recv()
+    lag = hops + 3
 
     def slot(step, carry):
         @pl.when(step < units)
@@ -435,6 +537,10 @@
                     g_copy(way, u_in, hops).wait_recv()
 
             project(u_in)
+
+        for later, work in ((1, merge), (2, activate)):
+            u_next = step - hops - later
+            pl.when((u_next >= 0) & (u_next < units))(functools.partial(work, u_next))
 
         u_mid = step - lag
 
@@ -470,12 +576,14 @@
     def drain(u, carry):
         rows_drain(u)
         ups_copy(u).wait_send()
-
-        @pl.when(u > 0)
-        def _():
-            back_copy(0, u).wait_send()
-
-        back_copy(1, u).wait_send()
+        twin_copy(u).wait_send()
+        act_copy(u).wait_send()
+        for b in (0, 1):
+
+            @pl.when((u > 0) | (c != b))
+            def _():
+                back_copy(b, u).wait_send()
+
         for way in (0, 1):
             for k in range(1, hops):
                 g_copy(way, u, k).wait_send()
@@ -489,6 +597,8 @@
         return carry
 
     lax.fori_loop(0, units, drain, 0)
+    for k in range(2 * chunks):
+        weight_copy(k).wait_send()
 
 
 def on_device(dims, *args):
@@ -497,7 +607,7 @@
     nz, nx, _ = dims
     units, hops = nz // 2, nx // 2
     count, width = stream.shape
-    hid = w_up.shape[1]
+    hid, narrow = w_up.shape[1], width // 2
     heads = key_rows.shape[1] // HD
     mine = nx * count
     stacked = width // nx // HD * mine
@@ -524,21 +634,29 @@
             pltpu.VMEM((stacked, HD), f32),
             pltpu.VMEM((stacked, HD), f32),
             pltpu.VMEM((stacked, HD), f32),
-            pltpu.VMEM((units, 2, count, width + META), bf16),
-            pltpu.VMEM((units, nx, count, width), bf16),
+            pltpu.VMEM((count, narrow + META), bf16),
+            pltpu.VMEM((units, 2, count, narrow + META), bf16),
+            pltpu.VMEM((units, nx, count, narrow), bf16),
             pltpu.VMEM((count, width), f32),
             pltpu.VMEM((2, count, META), f32),
-            pltpu.VMEM(w_up.shape, bf16),
-            pltpu.VMEM(w_down.shape, bf16),
+            pltpu.VMEM((narrow, hid), bf16),
+            pltpu.VMEM((hid, narrow), bf16),
+            pltpu.VMEM((narrow, hid), bf16),
+            pltpu.VMEM((hid, narrow), bf16),
             pltpu.VMEM((2, count, META), f32),
             pltpu.VMEM((2, count, META), f32),
             pltpu.VMEM((units, mine, hid), f32),
+            pltpu.VMEM((units, mine, hid), bf16),
+            pltpu.VMEM((units, mine, hid), bf16),
             pltpu.VMEM((units, mine, hid), f32),
-            pltpu.VMEM((units, nx, count, width), bf16),
-            pltpu.VMEM((2, units, hops, count, width), bf16),
-            pltpu.VMEM((2, units, hops, count, width), bf16),
-            pltpu.VMEM((units, 2, count // 2, width), bf16),
-            pltpu.VMEM((units, 2, count // 2, width), bf16),
+            pltpu.VMEM((units, mine, hid), f32),
+            pltpu.VMEM((units, mine, hid), bf16),
+            pltpu.VMEM((units, mine, hid), bf16),
+            pltpu.VMEM((units, nx, count, narrow), bf16),
+            pltpu.VMEM((2, units, hops, count, narrow), bf16),
+            pltpu.VMEM((2, units, hops, count, narrow), bf16),
+            pltpu.VMEM((units, 2, count // 2, narrow), bf16),
+            pltpu.VMEM((units, 2, count // 2, narrow), bf16),
             dma((2,)),
             dma((3, nx)),
             dma((3, nx)),
@@ -550,8 +668,10 @@
             dma((2, units)),
             dma((2,)),
             dma((2,)),
-            dma((units,)),
-            dma((units,)),
+            dma((3, units)),
+            dma((3, units)),
+            dma((2 * chunks,)),
+            dma((2 * chunks,)),
         ],
         compiler_params=pltpu.CompilerParams(
             collective_id=0, has_side_effects=True, vmem_limit_bytes=56 * 2**20

time: 176 us -> 181 us (1.028)
  Pallas kernels: 171 us -> 176 us
    pallas_call x1, Pallas kernels: 171 us -> 176 us  [on_device(): pl.pallas_call(functools.partial(kernel, dims), out_shape=(jax.ShapeDtype...]
where the time goes in v3:
time: 181 us
  Pallas kernels  176 us (97%)
  local copies, waits for them, and re-layouts  2.57 us (1%)
  between operations  1.93 us (1%)
    pallas_call x1, Pallas kernels, on_device(): pl.pallas_call(functools.partial(kernel, dims), out_shape=(jax.ShapeDtype...  176 us

profile of v3, /device:TPU:65, one launch (start us, length us, event | category | flops | bytes accessed | tf_op | source)
XLA Modules:
  0.0 180.8 jit_solution(17675837889509380194)
XLA Ops:
  1.9 176.3 %layer.1 = (bf16[8,3072]{1,0:T(8,128)(2,1)}, f32[1,128]{1,0:T(1,128)}) custom-call(bf16[8,3072]{1,0:T(8,128)(2,1)} %queries.1, bf16[8,512]{1,0:T(8,128)(2,1)} %key_rows.1, bf16[8,512]{1,0:T(8,128)(2,1)} %value_rows.1, bf16[8,3072]{1,0:T(8,128)(2,1)} %stream.1, s32[2,8]{1,0:T(2,128)} %bitcast.11, s32[1]{0:T(128)S(6)} %copy.16.seq_length, f32[1,3072]{1,0:T(1,128)} %bitcast.8, ...), custom_call_target="tpu_custom_call" | custom-call | tf_op jit(solution)/shard_map/layer/pallas_call | solution.py:620
  178.2 1.1 slice_bitcast_fusion
  179.4 1.4 copy.18

commit v4 on v3

--- a/solution.py
+++ b/solution.py
@@ -16,7 +16,7 @@
 GROUPS_SEQ = ("groups", "z", "x")
 eps = 1e-05
 masked = -1e30
-chunks = 4
+chunks = 8
 f32 = jnp.float32
 bf16 = jnp.bfloat16
 
@@ -58,16 +58,12 @@
     w_up,
     w_down,
     w_up_in,
-    w_down_in,
     stats,
     stats_in,
     ups,
     ups_out,
     ups_in,
-    ups_half,
     ups_twin,
-    act_out,
-    act_in,
     parts,
     sums,
     recv,
@@ -112,21 +108,14 @@
     m, pairs = z // 2, nz // 2
     narrow, hid = width // 2, w_up_hbm.shape[1]
     mate = {"z": z + 1 - 2 * c}
-    keep_cols = pl.ds(pl.multiple_of(c * narrow, HD), narrow)
-    give_cols = pl.ds(pl.multiple_of((1 - c) * narrow, HD), narrow)
-    up_copy = pltpu.make_async_copy(w_up_hbm.at[keep_cols, :], w_up, local_sem.at[0])
-    down_copy = pltpu.make_async_copy(w_down_hbm.at[:, keep_cols], w_down, local_sem.at[1])
+    keep_rows = pl.ds(pl.multiple_of(c * narrow, HD), narrow)
+    up_copy = pltpu.make_async_copy(w_up_hbm.at[keep_rows, :], w_up, local_sem.at[0])
+    down_copy = pltpu.make_async_copy(w_down_hbm, w_down, local_sem.at[1])
 
     def weight_copy(k):
-        if k < chunks:
-            size = narrow // chunks
-            at = pl.ds(pl.multiple_of((1 - c) * narrow + k * size, HD // 2), size)
-            return remote(
-                w_up_hbm.at[at, :], w_up_in.at[pl.ds(k * size, size), :], wsend.at[k], wrecv.at[k], mate
-            )
-        size = hid // chunks
-        at = pl.ds((k - chunks) * size, size)
-        return remote(w_down_hbm.at[at, give_cols], w_down_in.at[at, :], wsend.at[k], wrecv.at[k], mate)
+        size = narrow // chunks
+        at = pl.ds(pl.multiple_of((1 - c) * narrow + k * size, HD // 4), size)
+        return remote(w_up_hbm.at[at, :], w_up_in.at[pl.ds(k * size, size), :], wsend.at[k], wrecv.at[k], mate)
 
     up_copy.start()
     down_copy.start()
@@ -135,17 +124,20 @@
     def greet(peer):
         pl.semaphore_signal(barrier, inc=1, device_id=peer, device_id_type=pl.DeviceIdType.MESH)
 
+    kv[...] = jnp.zeros(kv.shape, bf16)
     for steps in (1, -1, 2, -2):
         greet(along_z(steps))
     for d in range(1, nx):
         greet({"x": lax.rem(x + d, nx)})
+    diagonal = {**mate, **twin}
     greet(twin)
+    greet(diagonal)
     for head in range(kv_width // HD):
         kv_own[head, :, :HD] = key_rows[:, head * HD : (head + 1) * HD]
         kv_own[head, :, HD:] = value_rows[:, head * HD : (head + 1) * HD]
     kv[0, 0, x] = kv_own[x // sharers]
     q_all[x] = queries[:, pl.ds(pl.multiple_of(x * q_width, HD), q_width)]
-    pl.semaphore_wait(barrier, 4 + nx)
+    pl.semaphore_wait(barrier, 5 + nx)
 
     def q_copy(d):
         peer = lax.rem(x + d, nx)
@@ -166,47 +158,43 @@
     for d in far_first:
         q_copy(d).start()
 
-    def z_ring(phase, at):
-        def first(way, u):
-            steps = (-u if u < 3 else -2) if way == 0 else min(u + 1, 2)
-            src = at(0, 0) if (u < 3 and way == 0) or u < 2 else at(u - 2, way)
-            return remote(src, at(u, way), zsend.at[way, u], zrecv.at[phase, way, u], along_z(steps))
-
-        def onward(way, u):
-            return remote(
-                at(u - 2, way), at(u, way), zsend.at[way, u], zrecv.at[phase, way, u],
-                along_z(-2 if way == 0 else 2),
-            )
-
-        def start():
-            for way, u in ((0, 2), (1, 1), (0, 1), (1, 0)):
-                first(way, u).start()
-
-        def take(u):
-            @pl.when(u > 0)
-            def _():
-                onward(0, u).wait_recv()
-
-                @pl.when(u + 2 < units)
-                def _():
-                    onward(0, u + 2).start()
-
-            onward(1, u).wait_recv()
-
-            @pl.when(u + 2 < units)
-            def _():
-                onward(1, u + 2).start()
-
-        def drain(u):
-            @pl.when(u > 0)
-            def _():
-                onward(0, u).wait_send()
-
-            onward(1, u).wait_send()
-
-        return start, take, drain
-
-    kv_start, kv_take, kv_drain = z_ring(0, lambda u, half: kv.at[lax.max(u, 0), half])
+    def wanted(way, u, steps):
+        at = lax.rem(z + nz + steps, nz)
+        if way == 1:
+            return at > u
+        return (at + u >= nz) | (u + 2 * (at // 2) + 2 < units)
+
+    def kv_copy_z(way, u, src, steps):
+        return remote(src, kv.at[u, way], zsend.at[0, way, u], zrecv.at[0, way, u], along_z(steps))
+
+    def kv_first(way, u):
+        steps = -u if way == 0 else u + 1
+        return kv_copy_z(way, u, kv.at[0, 0], steps), wanted(way, u, steps)
+
+    def kv_onward(way, u):
+        steps = -2 if way == 0 else 2
+        return kv_copy_z(way, u, kv.at[lax.max(u - 2, 0), way], steps), wanted(way, u, steps)
+
+    def kv_start():
+        for way, u in ((1, 1), (0, 2), (1, 0), (0, 1)):
+            copy, needed = kv_first(way, u)
+            pl.when(needed)(copy.start)
+
+    def kv_take(u):
+        for way in (1, 0):
+
+            @pl.when(wanted(way, u, 0) & ((u > 0) | (way == 1)))
+            def _():
+                kv_onward(way, u)[0].wait_recv()
+
+            copy, needed = kv_onward(way, u + 2)
+            pl.when(needed & (u + 2 < units) & ((u > 0) | (way == 1)))(copy.start)
+
+    def kv_drain(u):
+        for way in (0, 1):
+            steps = (-1 if way == 0 else 1) * jnp.minimum(u + way, 2)
+            pl.when(wanted(way, u, steps) & ((u > 0) | (way == 1)))(kv_onward(way, u)[0].wait_send)
+
     for d in range(1, nx):
         kv_copy(d).wait_recv()
     kv_start()
@@ -245,11 +233,11 @@
         mixed_values[...] = mixed_values[...] * keep + jnp.dot(p.astype(bf16), v, preferred_element_type=f32)
         return carry
 
-    each = 2 * chunks // units
     for u in range(units):
         attend(u, 0)
-        for k in range(u * each, (u + 1) * each):
-            weight_copy(k).start()
+    ahead = chunks - 3
+    for k in range(ahead):
+        weight_copy(k).start()
     attended = mixed_values[...] / weight_sum[...]
     for s in range(nx):
         for j in range(per):
@@ -258,14 +246,6 @@
     att_in[x] = att_out[x]
     for d in far_first:
         att_copy(d).start()
-    for d in range(1, nz):
-        greet(along_z(d))
-
-    def kv_sent(u, carry):
-        kv_drain(u)
-        return carry
-
-    lax.fori_loop(0, units, kv_sent, 0)
     for d in range(1, nx):
         kv_copy(d).wait_send()
         q_copy(d).wait_send()
@@ -315,11 +295,11 @@
     rows_z[0, c, :, narrow:] = place.astype(bf16)
 
     def mate_rows():
-        return remote(rows_out, rows_z.at[0, c], zsend.at[0, 0], zrecv.at[1, 0, 0], mate)
+        return remote(rows_out, rows_z.at[0, c], zsend.at[1, 0, 0], zrecv.at[1, 0, 0], mate)
 
     def rows_copy(b, u):
         return remote(
-            rows_z.at[lax.max(u - 2, 0), b], rows_z.at[u, b], zsend.at[b, u], zrecv.at[1, b, u],
+            rows_z.at[lax.max(u - 2, 0), b], rows_z.at[u, b], zsend.at[1, b, u], zrecv.at[1, b, u],
             along_z(2 - 4 * lax.rem(u, 2)),
         )
 
@@ -355,6 +335,7 @@
     info[0] = place
     info[1] = jnp.where(hit_a, gate_a, jnp.where(hit_b, gate_b, 0.0))
 
+    ringed, chained = units, units
     my_expert = z // (nz // EXPERTS)
     slots = count // 2
 
@@ -380,30 +361,39 @@
         )
 
     def ups_copy(u):
-        return remote(ups_out.at[u], ups_in.at[u], usend.at[0, u], urecv.at[0, u], mate)
+        return remote(ups_out.at[u], ups_in.at[0, u], usend.at[0, u], urecv.at[0, u], mate)
+
+    def cross_copy(u):
+        return remote(ups_out.at[u], ups_in.at[1, u], usend.at[3, u], urecv.at[3, u], diagonal)
 
     def twin_copy(u):
-        return remote(ups_half.at[u], ups_twin.at[u], usend.at[1, u], urecv.at[1, u], twin)
-
-    def act_copy(u):
-        return remote(act_out.at[u], act_in.at[u], usend.at[2, u], urecv.at[2, u], mate)
+        return remote(ups.at[u], ups_twin.at[u], usend.at[1, u], urecv.at[1, u], twin)
 
     def project(u):
         got = rows_x[u].reshape(mine, narrow)
         ups_out[u] = jnp.dot(got, w_up_in[...], preferred_element_type=f32).astype(bf16)
         ups_copy(u).start()
+        cross_copy(u).start()
         ups[u] = jnp.dot(got, w_up[...], preferred_element_type=f32)
-
-    def merge(u):
-        ups_copy(u).wait_recv()
-        ups_half[u] = ups[u] + ups_in[u].astype(f32)
         twin_copy(u).start()
 
-    def activate(u):
-        twin_copy(u).wait_recv()
-        v = ups_half[u] + ups_twin[u]
-        act_out[u] = (v / (1.0 + jnp.exp(-v))).astype(bf16)
-        act_copy(u).start()
+    def way_of(d):
+        return (0, d) if d <= hops else (1, nx - d)
+
+    def wide_copy(u, d):
+        way, h = way_of(d)
+        at = rows_x.at[u, x]
+        return remote(
+            at, at, xsend.at[0, way, u, h - 1], xrecv.at[0, way, u, h - 1], {"x": lax.rem(x + d, nx)}
+        )
+
+    def part_copy(u, d):
+        way, h = way_of(d)
+        peer = lax.rem(x + d, nx)
+        return remote(
+            parts.at[u, peer], recv.at[way, u, h - 1], xsend.at[1, way, u, h - 1], xrecv.at[1, way, u, h - 1],
+            {"x": peer},
+        )
 
     def own(way, u, k):
         ahead = hops - k
@@ -415,16 +405,27 @@
         )
 
     def expand(u):
-        act_copy(u).wait_recv()
-        made = jnp.dot(act_out[u], w_down[...], preferred_element_type=f32)
-        made = made + jnp.dot(act_in[u], w_down_in[...], preferred_element_type=f32)
+        ups_copy(u).wait_recv()
+        cross_copy(u).wait_recv()
+        twin_copy(u).wait_recv()
+        v = ups[u] + ups_twin[u] + (ups_in[0, u].astype(f32) + ups_in[1, u].astype(f32))
+        active = (v / (1.0 + jnp.exp(-v))).astype(bf16)
+        made = jnp.dot(active, w_down[...], preferred_element_type=f32)
         for d in range(nx):
             parts[u, d] = made[d * count : (d + 1) * count].astype(bf16)
-        for way in (0, 1):
-
-            @pl.when(lax.rem(u, 2) == way)
-            def _():
-                r_copy(way, u, 0, own(way, u, 0)).start()
+
+        @pl.when(u < chained)
+        def _():
+            for way in (0, 1):
+
+                @pl.when(lax.rem(u, 2) == way)
+                def _():
+                    r_copy(way, u, 0, own(way, u, 0)).start()
+
+        @pl.when(u >= chained)
+        def _():
+            for d in far_first:
+                part_copy(u, d).start()
 
     def offset(u):
         return ((u + 1) // 2) * (2 * lax.rem(u, 2) - 1)
@@ -438,11 +439,27 @@
         return remote(back_out.at[u, b], back_in.at[u, b], bsend.at[b, u], brecv.at[b, u], to)
 
     def home(u):
-        for way in (0, 1):
-            r_copy(way, u, hops - 1, own(way, u, hops - 1)).wait_recv()
-        both_ways = recv[0, u, hops - 1].astype(f32) + recv[1, u, hops - 1].astype(f32)
-        done = (parts[u, x].astype(f32) + both_ways).astype(bf16)
-
+        def settle(total):
+            done = total.astype(bf16)
+            back_in_or_out(u, done)
+
+        @pl.when(u < chained)
+        def _():
+            for way in (0, 1):
+                r_copy(way, u, hops - 1, own(way, u, hops - 1)).wait_recv()
+            both_ways = recv[0, u, hops - 1].astype(f32) + recv[1, u, hops - 1].astype(f32)
+            settle(parts[u, x].astype(f32) + both_ways)
+
+        @pl.when(u >= chained)
+        def _():
+            total = parts[u, x].astype(f32)
+            for d in range(1, nx):
+                part_copy(u, d).wait_recv()
+                way, h = way_of(d)
+                total = total + recv[way, u, h - 1].astype(f32)
+            settle(total)
+
+    def back_in_or_out(u, done):
         for b in (0, 1):
             back_out[u, b] = done[b * slots : (b + 1) * slots]
 
@@ -465,34 +482,73 @@
             def _():
                 back_arrival(b, u).wait_recv()
 
-            at = slice(b * narrow, (b + 1) * narrow)
             got = back_in[u, b].astype(f32)
-            mix = hidden[:, at]
+            mix = hidden[...]
             for i in range(slots):
                 mix = mix + weights[i] * got[i : i + 1]
-            hidden[:, at] = mix
+            hidden[...] = mix
 
     for d in range(1, nx):
         att_copy(d).wait_send()
     up_copy.wait()
     down_copy.wait()
-    pl.semaphore_wait(barrier, nz - 1)
-    for k in range(2 * chunks):
-        weight_copy(k).wait_recv()
-    lag = hops + 3
+    groups = ((0, units, hops, hops),)
+
+    def staged(step, delay, work):
+        for low, high, start, end in groups:
+            u = step - start - (delay if delay < 2 else delay - 1 + end)
+            pl.when((u >= low) & (u < high))(functools.partial(work, u))
+
+    def collect(u):
+        @pl.when(u < ringed)
+        def _():
+            for way in (0, 1):
+
+                @pl.when(lax.rem(u, 2) == way)
+                def _():
+                    g_copy(way, u, hops).wait_recv()
+
+        @pl.when(u >= ringed)
+        def _():
+            for d in range(1, nx):
+                way, h = way_of(d)
+                g_copy(way, u, h).wait_recv()
+
+        project(u)
+
+    first_project = min(hops, ringed + 1)
 
     def slot(step, carry):
         @pl.when(step < units)
         def _():
             rows_take(step)
             choose(step)
-            g_copy(0, step, 1).start()
-            g_copy(1, step, 1).start()
+
+            @pl.when(step == units - 1)
+            def _():
+                for d in range(1, nz):
+                    greet(along_z(d))
+
+            @pl.when(step < ringed)
+            def _():
+                g_copy(0, step, 1).start()
+                g_copy(1, step, 1).start()
+
+            @pl.when(step >= ringed)
+            def _():
+                for d in far_first:
+                    wide_copy(step, d).start()
+
+        for k in range(ahead, chunks):
+
+            @pl.when(step == max(0, first_project - 4) + k - ahead)
+            def _():
+                weight_copy(k).start()
 
         for h in range(1, hops):
             u = step - h
 
-            @pl.when((u >= 0) & (u < units))
+            @pl.when((u >= 0) & (u < ringed))
             def _():
                 for way in (0, 1):
                     g_copy(way, u, h).wait_recv()
@@ -505,9 +561,9 @@
                             g_copy(way, u, h + 1).start()
 
         for k in range(1, hops):
-            u = step - lag - k
-
-            @pl.when((u >= 0) & (u < units))
+            u = step - hops - 1 - k
+
+            @pl.when((u >= 0) & (u < chained))
             def _():
                 for way in (0, 1):
 
@@ -526,43 +582,25 @@
                         def _():
                             r_copy(way, u, k, own(way, u, k)).start()
 
-        u_in = step - hops
-
-        @pl.when((u_in >= 0) & (u_in < units))
-        def _():
-            for way in (0, 1):
-
-                @pl.when(lax.rem(u_in, 2) == way)
-                def _():
-                    g_copy(way, u_in, hops).wait_recv()
-
-            project(u_in)
-
-        for later, work in ((1, merge), (2, activate)):
-            u_next = step - hops - later
-            pl.when((u_next >= 0) & (u_next < units))(functools.partial(work, u_next))
-
-        u_mid = step - lag
-
-        @pl.when((u_mid >= 0) & (u_mid < units))
-        def _():
-            expand(u_mid)
-
-        u_out = step - lag - hops
-
-        @pl.when((u_out >= 0) & (u_out < units))
-        def _():
-            home(u_out)
-
-        u_last = step - lag - hops - 2
-
-        @pl.when(u_last >= 0)
-        def _():
-            blend(u_last)
-
+        first_home = min(low + start + 1 + end for low, high, start, end in groups)
+
+        @pl.when(step == first_home)
+        def _():
+            pl.semaphore_wait(barrier, nz - 1)
+
+        @pl.when(step == first_project)
+        def _():
+            for k in range(chunks):
+                weight_copy(k).wait_recv()
+
+        staged(step, 0, collect)
+        staged(step, 1, expand)
+        staged(step, 2, home)
+        staged(step, 4, blend)
         return carry
 
-    lax.fori_loop(0, units + lag + hops + 2, slot, 0)
+    last = max(high - 1 + start + 3 + end for low, high, start, end in groups)
+    lax.fori_loop(0, last + 1, slot, 0)
     out = hidden[...]
     layer_out[...] = out.astype(bf16)
     message = jnp.where(lane == 0, lane_sum(out * out), 0.0)
@@ -574,10 +612,11 @@
     values[...] = flat
 
     def drain(u, carry):
+        kv_drain(u)
         rows_drain(u)
         ups_copy(u).wait_send()
         twin_copy(u).wait_send()
-        act_copy(u).wait_send()
+        cross_copy(u).wait_send()
         for b in (0, 1):
 
             @pl.when((u > 0) | (c != b))
@@ -585,19 +624,21 @@
                 back_copy(b, u).wait_send()
 
         for way in (0, 1):
+            even = lax.rem(u, 2) == way
             for k in range(1, hops):
                 g_copy(way, u, k).wait_send()
+            for k in range(1, hops if way == 0 else hops - 1):
                 r_copy(way, u, k, own(way, u, k)).wait_send()
-
-            @pl.when(lax.rem(u, 2) == way)
-            def _():
-                g_copy(way, u, hops).wait_send()
-                r_copy(way, u, 0, own(way, u, 0)).wait_send()
+            one_way = (u < ringed) & even
+            pl.when(one_way | (u >= ringed) if way == 0 else one_way)(g_copy(way, u, hops).wait_send)
+            pl.when(((u < chained) & even) | (u >= chained))(r_copy(way, u, 0, own(way, u, 0)).wait_send)
+            if way == 1:
+                pl.when(u < chained)(r_copy(way, u, hops - 1, own(way, u, hops - 1)).wait_send)
 
         return carry
 
     lax.fori_loop(0, units, drain, 0)
-    for k in range(2 * chunks):
+    for k in range(chunks):
         weight_copy(k).wait_send()
 
 
@@ -640,27 +681,23 @@
             pltpu.VMEM((count, width), f32),
             pltpu.VMEM((2, count, META), f32),
             pltpu.VMEM((narrow, hid), bf16),
-            pltpu.VMEM((hid, narrow), bf16),
+            pltpu.VMEM((hid, width), bf16),
             pltpu.VMEM((narrow, hid), bf16),
-            pltpu.VMEM((hid, narrow), bf16),
             pltpu.VMEM((2, count, META), f32),
             pltpu.VMEM((2, count, META), f32),
             pltpu.VMEM((units, mine, hid), f32),
             pltpu.VMEM((units, mine, hid), bf16),
-            pltpu.VMEM((units, mine, hid), bf16),
+            pltpu.VMEM((2, units, mine, hid), bf16),
             pltpu.VMEM((units, mine, hid), f32),
-            pltpu.VMEM((units, mine, hid), f32),
-            pltpu.VMEM((units, mine, hid), bf16),
-            pltpu.VMEM((units, mine, hid), bf16),
-            pltpu.VMEM((units, nx, count, narrow), bf16),
-            pltpu.VMEM((2, units, hops, count, narrow), bf16),
-            pltpu.VMEM((2, units, hops, count, narrow), bf16),
-            pltpu.VMEM((units, 2, count // 2, narrow), bf16),
-            pltpu.VMEM((units, 2, count // 2, narrow), bf16),
+            pltpu.VMEM((units, nx, count, width), bf16),
+            pltpu.VMEM((2, units, hops, count, width), bf16),
+            pltpu.VMEM((2, units, hops, count, width), bf16),
+            pltpu.VMEM((units, 2, count // 2, width), bf16),
+            pltpu.VMEM((units, 2, count // 2, width), bf16),
             dma((2,)),
             dma((3, nx)),
             dma((3, nx)),
-            dma((2, units)),
+            dma((2, 2, units)),
             dma((2, 2, units)),
             dma((2, 2, units, hops)),
             dma((2, 2, units, hops)),
@@ -668,10 +705,10 @@
             dma((2, units)),
             dma((2,)),
             dma((2,)),
-            dma((3, units)),
-            dma((3, units)),
-            dma((2 * chunks,)),
-            dma((2 * chunks,)),
+            dma((4, units)),
+            dma((4, units)),
+            dma((chunks,)),
+            dma((chunks,)),
         ],
         compiler_params=pltpu.CompilerParams(
             collective_id=0, has_side_effects=True, vmem_limit_bytes=56 * 2**20

time: 181 us -> 171 us (0.945)
  Pallas kernels: 176 us -> 167 us
    pallas_call x1, Pallas kernels: 176 us -> 167 us  [on_device(): pl.pallas_call(functools.partial(kernel, dims), out_shape=(jax.ShapeDtype...]
where the time goes in v4:
time: 171 us
  Pallas kernels  167 us (98%)
  local copies, waits for them, and re-layouts  2.57 us (2%)
  between operations  1.93 us (1%)
    pallas_call x1, Pallas kernels, on_device(): pl.pallas_call(functools.partial(kernel, dims), out_shape=(jax.ShapeDtype...  167 us

profile of v4, /device:TPU:65, one launch (start us, length us, event | category | flops | bytes accessed | tf_op | source)
XLA Modules:
  0.0 171.2 jit_solution(8470240074048159358)
XLA Ops:
  1.9 166.7 %layer.1 = (bf16[8,3072]{1,0:T(8,128)(2,1)}, f32[1,128]{1,0:T(1,128)}) custom-call(bf16[8,3072]{1,0:T(8,128)(2,1)} %queries.1, bf16[8,512]{1,0:T(8,128)(2,1)} %key_rows.1, bf16[8,512]{1,0:T(8,128)(2,1)} %value_rows.1, bf16[8,3072]{1,0:T(8,128)(2,1)} %stream.1, s32[2,8]{1,0:T(2,128)} %bitcast.11, s32[1]{0:T(128)S(6)} %copy.16.seq_length, f32[1,3072]{1,0:T(1,128)} %bitcast.8, ...), custom_call_target="tpu_custom_call" | custom-call | tf_op jit(solution)/shard_map/layer/pallas_call | solution.py:661
  168.6 1.1 slice_bitcast_fusion
  169.7 1.4 copy.18

commit v5 on v4

--- a/solution.py
+++ b/solution.py
@@ -596,10 +596,10 @@
         staged(step, 0, collect)
         staged(step, 1, expand)
         staged(step, 2, home)
-        staged(step, 4, blend)
+        staged(step, 6, blend)
         return carry
 
-    last = max(high - 1 + start + 3 + end for low, high, start, end in groups)
+    last = max(high - 1 + start + 5 + end for low, high, start, end in groups)
     lax.fori_loop(0, last + 1, slot, 0)
     out = hidden[...]
     layer_out[...] = out.astype(bf16)

time: 171 us -> 171 us (level)
  no operation moved by 1% of the time
where the time goes in v5:
time: 171 us
  Pallas kernels  167 us (98%)
  local copies, waits for them, and re-layouts  2.57 us (2%)
  between operations  1.93 us (1%)
    pallas_call x1, Pallas kernels, on_device(): pl.pallas_call(functools.partial(kernel, dims), out_shape=(jax.ShapeDtype...  167 us

profile of v5, /device:TPU:65, one launch (start us, length us, event | category | flops | bytes accessed | tf_op | source)
XLA Modules:
  0.0 171.2 jit_solution(12897472812875771600)
XLA Ops:
  1.9 166.7 %layer.1 = (bf16[8,3072]{1,0:T(8,128)(2,1)}, f32[1,128]{1,0:T(1,128)}) custom-call(bf16[8,3072]{1,0:T(8,128)(2,1)} %queries.1, bf16[8,512]{1,0:T(8,128)(2,1)} %key_rows.1, bf16[8,512]{1,0:T(8,128)(2,1)} %value_rows.1, bf16[8,3072]{1,0:T(8,128)(2,1)} %stream.1, s32[2,8]{1,0:T(2,128)} %bitcast.11, s32[1]{0:T(128)S(6)} %copy.16.seq_length, f32[1,3072]{1,0:T(1,128)} %bitcast.8, ...), custom_call_target="tpu_custom_call" | custom-call | tf_op jit(solution)/shard_map/layer/pallas_call | solution.py:661
  168.6 1.1 slice_bitcast_fusion
  169.7 1.4 copy.18
